TPU v7x, 32 devices: a whole 2x2x4 slice. The times are simulated.
32 devices in a mesh: comp: 2 (over x), tile: 16 (over z, y, core).
Axes of the slice: x: 2, y: 2, z: 4, core: 2. Of those that a mesh axis runs over, the one named last changes fastest.
Arguments:
- starting_perturbation: float32 [2, 128, 128, 512], P('comp', None, 'tile'), may hold values from -6 to 6
- measured_discrepancy: float32 [2, 128, 128, 512], P('comp', None, 'tile'), may hold values from -6 to 6
- diffusion: float32 [2, 128, 128, 512], P('comp', None, 'tile'), may hold values from 0.02 to 0.24
- vert_mix: float32 [2, 128, 128], P('comp'), may hold values from -0.03125 to 0.03125
- ocean_mask: int32 [128, 512], P('tile'), may hold values 0 or 1
- pair_tile: int32 [2, 16, 8], replicated, may hold values from 0 to 15, as said below
- pair_patch: int32 [2, 16, 64], replicated, may hold values from 0 to 31
- dest_patch: int32 [2, 16, 64], P('comp', 'tile'), may hold values from 0 to 31
- pair_blocks: int32 [2, 16, 8], P('comp', 'tile'), may hold values from 1 to 8, 48 in all within a row
- remap_weight: float32 [2, 1024, 128, 128], P('comp', 'tile'), may hold values from -0.5 to 0.5
Outputs:
- final_perturbation: float32 [2, 128, 128, 512], P('comp', None, 'tile')
- gradient: float32 [2, 128, 128, 512], P('comp', None, 'tile')
Inputs may be any that keep to these rules, and one draw needn't show every extreme that they name: `pair_tile`: the 8 source tiles listed for destination tile t are distinct; exactly one of them is (t + 8) mod 16, and each other is (t + o) mod 16 for some o from 1 - 8 to 7. A pair's live blocks are its first pair_blocks ones.
All inputs are finite; a program needn't handle non-finite values. No bound on the sum of `ocean_mask` on one device may be relied on, other than what follows from the above.
Results may differ from a plain program's by a relative error of at most 0.0001.
Values sent between devices are 32-bit elements; how exact they have to be, the bound alone decides.
A program may use at most 128 MiB of HBM per device.

v0:
```python
import jax
import jax.numpy as jnp
from jax import lax
from jax.sharding import PartitionSpec as P

STEPS = 4


precise = lax.Precision.HIGHEST


def partner_2(value, axis, distance):
    mask = 2**distance
    pairs = [(source, source ^ mask) for source in range(lax.axis_size(axis))]
    return lax.ppermute(value, axis, pairs)


def with_halo(x, sides, width):
    for axis, dim in sides:
        devices, length = (lax.axis_size(axis), x.shape[dim])
        up = [(i, (i + 1) % devices) for i in range(devices - 1)]
        down = [(j, i) for i, j in up]
        last = lax.slice_in_dim(x, length - width, length, axis=dim)
        first = lax.slice_in_dim(x, 0, width, axis=dim)
        before = lax.ppermute(last, axis, up)
        after = lax.ppermute(first, axis, down)
        x = jnp.concatenate([before, x, after], axis=dim)
    return x


def side_sum(interior):
    return jnp.roll(interior, -1, axis=3) + jnp.roll(interior, 1, axis=3) - 4.0 * interior


def column_mix(matrix, system_variables):
    return jnp.einsum("clm,cmrx->clrx", matrix, system_variables, precision=precise)


def shards(
    starting_perturbation,
    measured_discrepancy,
    diffusion,
    vert_mix,
    ocean_mask,
    pair_tile,
    pair_patch,
    dest_patch,
    pair_blocks,
    remap_weight,
):
    component = lax.axis_index("comp")
    own_tile = lax.axis_index("tile")
    tile_count = lax.axis_size("tile")
    row_count = starting_perturbation.shape[2]
    lon_count = starting_perturbation.shape[3]
    patch_len = remap_weight.shape[2]
    patch_count = row_count * lon_count // patch_len
    block_count = remap_weight.shape[1]
    pair_count = pair_tile.shape[2]
    per_pair = block_count // pair_count
    partner = 1 - component
    seawater_indicator = jnp.where(component == 1, ocean_mask.astype(jnp.float32), 1.0)[None, None]
    mix_back = jnp.swapaxes(vert_mix, 1, 2)
    block_ids = jnp.arange(block_count, dtype=jnp.int32)
    slot_ids = block_ids % per_pair
    own_tiles = jnp.repeat(pair_tile[component, own_tile], per_pair)
    live_mask = (slot_ids < jnp.repeat(pair_blocks[0, 0], per_pair)).astype(jnp.float32)[:, None]
    landing = (
        dest_patch[0, 0][:, None] == jnp.arange(patch_count, dtype=jnp.int32)[None, :]
    ).astype(jnp.float32)
    weights = remap_weight[0]
    hit_table = (pair_tile[partner] == own_tile).astype(jnp.int32)
    feed_table = pair_patch[partner].reshape(tile_count, pair_count, per_pair)
    send_rows = jnp.sum(hit_table[:, :, None] * feed_table, axis=1)
    sent_mask = jnp.sum(hit_table, axis=1).astype(jnp.float32)[:, None, None]

    def tile_propagator_step(system_variables):
        for step_index in range(STEPS):
            padded = with_halo(system_variables, (("tile", 2),), 1)
            laplace = padded[:, :, 2:] + padded[:, :, :-2] + side_sum(system_variables)
            system_variables = seawater_indicator * (
                system_variables + diffusion * laplace + column_mix(vert_mix, system_variables)
            )
        return system_variables

    def backward_block(adjoint):
        for step_index in range(STEPS):
            masked = seawater_indicator * adjoint
            scaled = diffusion * masked
            padded = with_halo(scaled, (("tile", 2),), 1)
            adjoint = (
                masked
                + padded[:, :, 2:]
                + padded[:, :, :-2]
                + side_sum(scaled)
                + column_mix(mix_back, masked)
            )
        return adjoint

    system_variables = tile_propagator_step(starting_perturbation)
    surface = system_variables[0, 0].reshape(patch_count, patch_len)
    outgoing = surface[send_rows] * sent_mask
    crossed = partner_2(outgoing, "comp", 0)
    arrived = lax.all_to_all(crossed, "tile", split_axis=0, concat_axis=0, tiled=True)
    picked = arrived.reshape(tile_count * per_pair, patch_len)[own_tiles * per_pair + slot_ids]
    block_terms = jnp.einsum("bij,bj->bi", weights, picked, precision=precise) * live_mask
    summed_sensitivity = jnp.dot(landing.T, block_terms, precision=precise).reshape(
        row_count, lon_count
    )
    final_perturbation = tile_propagator_step(
        system_variables.at[0, 0].add(seawater_indicator[0, 0] * summed_sensitivity)
    )
    measurement_mismatch = final_perturbation - measured_discrepancy
    adjoint = backward_block(measurement_mismatch)
    masked = (seawater_indicator[0, 0] * adjoint[0, 0]).reshape(patch_count, patch_len)
    spread = jnp.dot(landing, masked, precision=precise)
    backpropagated_sensitivity = (
        jnp.einsum("bji,bj->bi", weights, spread, precision=precise) * live_mask
    )
    parcel = (
        jnp.zeros((tile_count, per_pair, patch_len), jnp.float32)
        .at[own_tiles, slot_ids]
        .add(backpropagated_sensitivity)
    )
    collected = lax.all_to_all(parcel, "tile", split_axis=0, concat_axis=0, tiled=True)
    crossed = partner_2(collected, "comp", 0)
    returned = (
        jnp.zeros((patch_count, patch_len), jnp.float32)
        .at[send_rows.reshape(-1)]
        .add((crossed * sent_mask).reshape(tile_count * per_pair, patch_len))
    )
    gradient_vector_output = backward_block(
        adjoint.at[0, 0].add(returned.reshape(row_count, lon_count))
    )
    return (final_perturbation, starting_perturbation + gradient_vector_output)


def solution(mesh):
    placed = (
        P("comp", None, "tile", None),
        P("comp", None, "tile", None),
        P("comp", None, "tile", None),
        P("comp", None, None),
        P("tile", None),
        P(),
        P(),
        P("comp", "tile", None),
        P("comp", "tile", None),
        P("comp", "tile", None, None),
    )
    return jax.shard_map(
        shards,
        mesh=mesh,
        in_specs=placed,
        out_specs=(P("comp", None, "tile", None), P("comp", None, "tile", None)),
        check_vma=False,
    )
```

profile of v0, /device:TPU:1, one launch (start us, length us, event | category | flops | bytes accessed | tf_op | source)
XLA Modules:
  0.0 343.1 jit_solution(11287301050036643213)
XLA Ops:
  0.6 2.8 copy.88
  5.5 4.5 %collective-permute-start.1 = (f32[1,128,1,512]{3,1,2,0:T(8,128)S(1)}, f32[1,128,1,512]{3,1,2,0:T(8,128)S(1)}, u32[]{:S(2)}, u32[]{:S(2)}) collective-permute-start(f32[1,128,1,512]{3,1,2,0:T(8,128)S(1)} %get-tuple-element.127), channel_id=1, source_target_pairs={{0,1},{1,2},{2,3},{3,4},{4,5},{5,6},{6,7},{7,8},{8,9},{9,10},{10,1... | collective-permute-start | bytes 786440 | tf_op jit(solution)/shard_map/ppermute | solution.py:25
  10.1 2.8 fusion.281
  15.1 9.9 %fusion.90 = f32[1,128,8,512]{3,1,2,0:T(8,128)S(1)} fusion(f32[1,128,8,512]{3,1,2,0:T(8,128)} %copy-done.4, f32[1,128,1,512]{3,1,2,0:T(8,128)S(1)} %collective-permute-done.1, f32[1,128,1,512]{3,1,2,0:T(8,128)S(1)} %collective-permute-done, f32[1,128,8,1]{3,1,2,0:T(8,128)S(1)} %get-tuple-element.123, f32[1,128,8,511]{3,1,2,0:T(8,128)} %get-tuple-element.125, ...), kind=kOutput, calls=%fused_computation.125 | convolution fusion | flops 812122112 | bytes 13189120 | tf_op jit(solution)/shard_map/clm,cmrx->clrx/dot_general | solution.py:36
  27.8 4.6 %collective-permute-start.3 = (f32[1,128,1,512]{3,1,2,0:T(8,128)S(1)}, f32[1,128,1,512]{3,1,2,0:T(8,128)S(1)}, u32[]{:S(2)}, u32[]{:S(2)}) collective-permute-start(f32[1,128,1,512]{3,1,2,0:T(8,128)S(1)} %get-tuple-element.121), channel_id=1, source_target_pairs={{0,1},{1,2},{2,3},{3,4},{4,5},{5,6},{6,7},{7,8},{8,9},{9,10},{10,1... | collective-permute-start | bytes 786440 | tf_op jit(solution)/shard_map/ppermute | solution.py:25
  34.3 3.1 collective-permute-done.3
  37.4 4.6 %fusion.84 = f32[1,128,8,512]{3,1,2,0:T(8,128)S(1)} fusion(f32[1,128,8,512]{3,1,2,0:T(8,128)S(1)} %fusion.90, f32[1,128,1,512]{3,1,2,0:T(8,128)S(1)} %collective-permute-done.3, f32[1,128,1,512]{3,1,2,0:T(8,128)S(1)} %collective-permute-done.2, f32[1,128,8,1]{3,1,2,0:T(8,128)S(1)} %get-tuple-element.117, f32[1,128,8,511]{3,1,2,0:T(8,128)S(1)} %get-tuple-element.119, ...), kind=kOutput, calls=%fused_computation.117 | convolution fusion | flops 812122112 | bytes 11091968 | tf_op jit(solution)/shard_map/clm,cmrx->clrx/dot_general | solution.py:36
  44.7 4.4 %collective-permute-start.5 = (f32[1,128,1,512]{3,1,2,0:T(8,128)S(1)}, f32[1,128,1,512]{3,1,2,0:T(8,128)S(1)}, u32[]{:S(2)}, u32[]{:S(2)}) collective-permute-start(f32[1,128,1,512]{3,1,2,0:T(8,128)S(1)} %get-tuple-element.115), channel_id=1, source_target_pairs={{0,1},{1,2},{2,3},{3,4},{4,5},{5,6},{6,7},{7,8},{8,9},{9,10},{10,1... | collective-permute-start | bytes 786440 | tf_op jit(solution)/shard_map/ppermute | solution.py:25
  53.3 4.6 %fusion.78 = f32[1,128,8,512]{3,1,2,0:T(8,128)S(1)} fusion(f32[1,128,8,512]{3,1,2,0:T(8,128)S(1)} %fusion.84, f32[1,128,1,512]{3,1,2,0:T(8,128)S(1)} %collective-permute-done.5, f32[1,128,1,512]{3,1,2,0:T(8,128)S(1)} %collective-permute-done.4, f32[1,128,8,1]{3,1,2,0:T(8,128)S(1)} %get-tuple-element.111, f32[1,128,8,511]{3,1,2,0:T(8,128)S(1)} %get-tuple-element.113, ...), kind=kOutput, calls=%fused_computation.109 | convolution fusion | flops 812122112 | bytes 11091968 | tf_op jit(solution)/shard_map/clm,cmrx->clrx/dot_general | solution.py:36
  60.7 4.6 %collective-permute-start.7 = (f32[1,128,1,512]{3,1,2,0:T(8,128)S(1)}, f32[1,128,1,512]{3,1,2,0:T(8,128)S(1)}, u32[]{:S(2)}, u32[]{:S(2)}) collective-permute-start(f32[1,128,1,512]{3,1,2,0:T(8,128)S(1)} %get-tuple-element.109), channel_id=1, source_target_pairs={{0,1},{1,2},{2,3},{3,4},{4,5},{5,6},{6,7},{7,8},{8,9},{9,10},{10,1... | collective-permute-start | bytes 786440 | tf_op jit(solution)/shard_map/ppermute | solution.py:25
  69.4 4.6 %fusion.72 = f32[1,128,8,512]{3,1,2,0:T(8,128)S(1)} fusion(f32[1,128,8,512]{3,1,2,0:T(8,128)S(1)} %fusion.78, f32[1,128,1,512]{3,1,2,0:T(8,128)S(1)} %collective-permute-done.7, f32[1,128,1,512]{3,1,2,0:T(8,128)S(1)} %collective-permute-done.6, f32[1,128,8,1]{3,1,2,0:T(8,128)S(1)} %get-tuple-element.105, f32[1,128,8,511]{3,1,2,0:T(8,128)S(1)} %get-tuple-element.107, ...), kind=kOutput, calls=%fused_computation.101 | convolution fusion | flops 812122112 | bytes 11091968 | tf_op jit(solution)/shard_map/clm,cmrx->clrx/dot_general | solution.py:36
  79.3 7.2 %all-to-all-start = ((f32[16,8,128]{2,1,0:T(8,128)}), f32[16,8,128]{2,1,0:T(8,128)S(1)}, u32[]{:S(2)}, u32[]{:S(2)}) async-start(f32[16,8,128]{2,1,0:T(8,128)} %collective-permute-done.8), calls=%async_computation | async-start | bytes 131072 | tf_op jit(solution)/shard_map/all_to_all | solution.py:104
  86.6 6.0 %all-to-all-done = f32[16,8,128]{2,1,0:T(8,128)S(1)} async-done(((f32[16,8,128]{2,1,0:T(8,128)}), f32[16,8,128]{2,1,0:T(8,128)S(1)}, u32[]{:S(2)}, u32[]{:S(2)}) %all-to-all-start) | async-done | bytes 65568 | tf_op jit(solution)/shard_map/all_to_all | solution.py:104
  93.2 8.3 %fusion.2 = f32[64,1,128]{2,1,0:T(1,128)S(1)} fusion(f32[64,128,1]{1,2,0:T(1,128)S(1)} %bitcast.279, f32[1,64,128,128]{3,2,1,0:T(8,128)} %param.23), kind=kOutput, calls=%fused_computation.6 | convolution fusion | flops 12582912 | bytes 4259840 | tf_op jit(solution)/shard_map/bij,bj->bi/dot_general | solution.py:106
  103.5 3.1 fusion.269
  106.7 2.6 collective-permute-start.10
  112.6 4.4 %collective-permute-done.9 = f32[1,128,1,512]{3,1,2,0:T(8,128)S(1)} collective-permute-done((f32[1,128,1,512]{3,1,2,0:T(8,128)S(1)}, f32[1,128,1,512]{3,1,2,0:T(8,128)S(1)}, u32[]{:S(2)}, u32[]{:S(2)}) %collective-permute-start.9) | collective-permute-done | bytes 262176 | tf_op jit(solution)/shard_map/ppermute | solution.py:26
  117.0 4.6 %fusion.66 = f32[1,128,8,512]{3,1,2,0:T(8,128)S(1)} fusion(f32[1,128,8,512]{3,1,2,0:T(8,128)S(1)} %copy-done.3, f32[1,128,1,512]{3,1,2,0:T(8,128)S(1)} %collective-permute-done.10, f32[1,128,1,512]{3,1,2,0:T(8,128)S(1)} %collective-permute-done.9, f32[1,128,8,1]{3,1,2,0:T(8,128)S(1)} %get-tuple-element.99, f32[1,128,8,511]{3,1,2,0:T(8,128)S(1)} %get-tuple-element.101, ...), kind=kOutput, calls=%fused_computation.93 | convolution fusion | flops 812122112 | bytes 11091968 | tf_op jit(solution)/shard_map/clm,cmrx->clrx/dot_general | solution.py:36
  124.3 3.6 %collective-permute-start.12 = (f32[1,128,1,512]{3,1,2,0:T(8,128)S(1)}, f32[1,128,1,512]{3,1,2,0:T(8,128)S(1)}, u32[]{:S(2)}, u32[]{:S(2)}) collective-permute-start(f32[1,128,1,512]{3,1,2,0:T(8,128)S(1)} %get-tuple-element.97), channel_id=1, source_target_pairs={{0,1},{1,2},{2,3},{3,4},{4,5},{5,6},{6,7},{7,8},{8,9},{9,10},{10,1... | collective-permute-start | bytes 786440 | tf_op jit(solution)/shard_map/ppermute | solution.py:25
  130.1 3.9 %collective-permute-done.12 = f32[1,128,1,512]{3,1,2,0:T(8,128)S(1)} collective-permute-done((f32[1,128,1,512]{3,1,2,0:T(8,128)S(1)}, f32[1,128,1,512]{3,1,2,0:T(8,128)S(1)}, u32[]{:S(2)}, u32[]{:S(2)}) %collective-permute-start.12) | collective-permute-done | bytes 262176 | tf_op jit(solution)/shard_map/ppermute | solution.py:25
  134.0 4.6 %fusion.60 = f32[1,128,8,512]{3,1,2,0:T(8,128)S(1)} fusion(f32[1,128,8,512]{3,1,2,0:T(8,128)S(1)} %fusion.66, f32[1,128,1,512]{3,1,2,0:T(8,128)S(1)} %collective-permute-done.12, f32[1,128,1,512]{3,1,2,0:T(8,128)S(1)} %collective-permute-done.11, f32[1,128,8,1]{3,1,2,0:T(8,128)S(1)} %get-tuple-element.93, f32[1,128,8,511]{3,1,2,0:T(8,128)S(1)} %get-tuple-element.95, ...), kind=kOutput, calls=%fused_computation.85 | convolution fusion | flops 812122112 | bytes 11091968 | tf_op jit(solution)/shard_map/clm,cmrx->clrx/dot_general | solution.py:36
  141.3 4.6 %collective-permute-start.14 = (f32[1,128,1,512]{3,1,2,0:T(8,128)S(1)}, f32[1,128,1,512]{3,1,2,0:T(8,128)S(1)}, u32[]{:S(2)}, u32[]{:S(2)}) collective-permute-start(f32[1,128,1,512]{3,1,2,0:T(8,128)S(1)} %get-tuple-element.91), channel_id=1, source_target_pairs={{0,1},{1,2},{2,3},{3,4},{4,5},{5,6},{6,7},{7,8},{8,9},{9,10},{10,1... | collective-permute-start | bytes 786440 | tf_op jit(solution)/shard_map/ppermute | solution.py:25
  149.9 4.6 %fusion.54 = f32[1,128,8,512]{3,1,2,0:T(8,128)S(1)} fusion(f32[1,128,8,512]{3,1,2,0:T(8,128)S(1)} %fusion.60, f32[1,128,1,512]{3,1,2,0:T(8,128)S(1)} %collective-permute-done.14, f32[1,128,1,512]{3,1,2,0:T(8,128)S(1)} %collective-permute-done.13, f32[1,128,8,1]{3,1,2,0:T(8,128)S(1)} %get-tuple-element.87, f32[1,128,8,511]{3,1,2,0:T(8,128)S(1)} %get-tuple-element.89, ...), kind=kOutput, calls=%fused_computation.77 | convolution fusion | flops 812122112 | bytes 11091968 | tf_op jit(solution)/shard_map/clm,cmrx->clrx/dot_general | solution.py:36
  157.4 4.4 %collective-permute-start.16 = (f32[1,128,1,512]{3,1,2,0:T(8,128)S(1)}, f32[1,128,1,512]{3,1,2,0:T(8,128)S(1)}, u32[]{:S(2)}, u32[]{:S(2)}) collective-permute-start(f32[1,128,1,512]{3,1,2,0:T(8,128)S(1)} %get-tuple-element.85), channel_id=1, source_target_pairs={{0,1},{1,2},{2,3},{3,4},{4,5},{5,6},{6,7},{7,8},{8,9},{9,10},{10,1... | collective-permute-start | bytes 786440 | tf_op jit(solution)/shard_map/ppermute | solution.py:25
  166.0 5.6 %copy_multiply_fusion.6 = (f32[1,128,8,512]{3,1,2,0:T(8,128)S(1)}, f32[1,128,8,512]{3,1,2,0:T(8,128)S(1)}) fusion(f32[1,128,8,512]{3,2,1,0:T(8,128)S(1)} %copy-done.1, f32[1,128,8,512]{3,2,1,0:T(8,128)S(1)} %copy-done.9, f32[8,512]{1,0:T(8,128)S(1)} %convert_select_fusion, f32[1,128,128]{2,1,0:T(8,128)S(1)} %copy-done, f32[1,128,8,512]{3,1,2,0:T(8,128)S(1)} %fusion.54, ...), kind=kOutput, calls=%fused_computation.202 | convolution fusion | flops 813694976 | bytes 15286272 | tf_op jit(solution)/shard_map/clm,cmrx->clrx/dot_general | solution.py:36
  174.5 4.4 %collective-permute-start.18 = (f32[1,128,1,512]{3,1,2,0:T(8,128)S(1)}, f32[1,128,1,512]{3,1,2,0:T(8,128)S(1)}, u32[]{:S(2)}, u32[]{:S(2)}) collective-permute-start(f32[1,128,1,512]{3,1,2,0:T(8,128)S(1)} %get-tuple-element.79), channel_id=1, source_target_pairs={{0,1},{1,2},{2,3},{3,4},{4,5},{5,6},{6,7},{7,8},{8,9},{9,10},{10,1... | collective-permute-start | bytes 786440 | tf_op jit(solution)/shard_map/ppermute | solution.py:25
  182.9 7.1 %copy_multiply_fusion.5 = (f32[1,128,8,512]{3,1,2,0:T(8,128)S(1)}, f32[1,128,8,512]{3,1,2,0:T(8,128)S(1)}) fusion(f32[1,128,8,512]{3,2,1,0:T(8,128)S(1)} %copy-done.1, f32[1,128,128]{2,1,0:T(8,128)S(1)} %copy-done, f32[1,128,8,512]{3,1,2,0:T(8,128)S(1)} %get-tuple-element.131, f32[1,128,8,512]{3,2,1,0:T(8,128)S(1)} %copy-done.9, ...), kind=kOutput, calls=%fused_computation.201 | convolution fusion | flops 814219264 | bytes 17383424 | tf_op jit(solution)/shard_map/clm,cmrx->clrx/dot_general | solution.py:36
  192.7 4.8 %collective-permute-start.20 = (f32[1,128,1,512]{3,1,2,0:T(8,128)S(1)}, f32[1,128,1,512]{3,1,2,0:T(8,128)S(1)}, u32[]{:S(2)}, u32[]{:S(2)}) collective-permute-start(f32[1,128,1,512]{3,1,2,0:T(8,128)S(1)} %get-tuple-element.73), channel_id=1, source_target_pairs={{0,1},{1,2},{2,3},{3,4},{4,5},{5,6},{6,7},{7,8},{8,9},{9,10},{10,1... | collective-permute-start | bytes 786440 | tf_op jit(solution)/shard_map/ppermute | solution.py:25
  201.5 4.7 %copy_multiply_fusion.4 = (f32[1,128,8,512]{3,1,2,0:T(8,128)S(1)}, f32[1,128,8,512]{3,1,2,0:T(8,128)S(1)}) fusion(f32[1,128,8,512]{3,2,1,0:T(8,128)S(1)} %copy-done.1, f32[1,128,128]{2,1,0:T(8,128)S(1)} %copy-done, f32[1,128,8,512]{3,1,2,0:T(8,128)S(1)} %get-tuple-element.133, f32[1,128,8,512]{3,1,2,0:T(8,128)S(1)} %get-tuple-element.132, ...), kind=kOutput, calls=%fused_computation.200 | convolution fusion | flops 812122112 | bytes 15286272 | tf_op jit(solution)/shard_map/clm,cmrx->clrx/dot_general | solution.py:36
  208.9 4.4 %collective-permute-start.22 = (f32[1,128,1,512]{3,1,2,0:T(8,128)S(1)}, f32[1,128,1,512]{3,1,2,0:T(8,128)S(1)}, u32[]{:S(2)}, u32[]{:S(2)}) collective-permute-start(f32[1,128,1,512]{3,1,2,0:T(8,128)S(1)} %get-tuple-element.67), channel_id=1, source_target_pairs={{0,1},{1,2},{2,3},{3,4},{4,5},{5,6},{6,7},{7,8},{8,9},{9,10},{10,1... | collective-permute-start | bytes 786440 | tf_op jit(solution)/shard_map/ppermute | solution.py:25
  217.5 4.7 %copy_multiply_fusion.3 = (f32[1,128,8,512]{3,1,2,0:T(8,128)S(1)}, f32[1,128,8,512]{3,1,2,0:T(8,128)S(1)}) fusion(f32[1,128,8,512]{3,2,1,0:T(8,128)S(1)} %copy-done.1, f32[1,128,128]{2,1,0:T(8,128)S(1)} %copy-done, f32[1,128,8,512]{3,1,2,0:T(8,128)S(1)} %get-tuple-element.135, f32[1,128,8,512]{3,1,2,0:T(8,128)S(1)} %get-tuple-element.134, ...), kind=kOutput, calls=%fused_computation.199 | convolution fusion | flops 812122112 | bytes 15286272 | tf_op jit(solution)/shard_map/clm,cmrx->clrx/dot_general | solution.py:36
  225.1 4.6 %collective-permute-start.24 = (f32[1,128,1,512]{3,1,2,0:T(8,128)S(1)}, f32[1,128,1,512]{3,1,2,0:T(8,128)S(1)}, u32[]{:S(2)}, u32[]{:S(2)}) collective-permute-start(f32[1,128,1,512]{3,1,2,0:T(8,128)S(1)} %get-tuple-element.61), channel_id=1, source_target_pairs={{0,1},{1,2},{2,3},{3,4},{4,5},{5,6},{6,7},{7,8},{8,9},{9,10},{10,1... | collective-permute-start | bytes 786440 | tf_op jit(solution)/shard_map/ppermute | solution.py:25
  233.7 3.7 %fusion.26 = f32[1,128,8,512]{3,1,2,0:T(8,128)S(1)} fusion(f32[1,128,8,512]{3,1,2,0:T(8,128)S(1)} %get-tuple-element.136, f32[1,128,1,512]{3,1,2,0:T(8,128)S(1)} %collective-permute-done.24, f32[1,128,8,512]{3,1,2,0:T(8,128)S(1)} %get-tuple-element.137, f32[1,128,1,512]{3,1,2,0:T(8,128)S(1)} %collective-permute-done.23, ...), kind=kOutput, calls=%fused_computation.39 | convolution fusion | flops 811073536 | bytes 11075584 | tf_op jit(solution)/shard_map/clm,cmrx->clrx/dot_general | solution.py:36
  238.9 5.3 %fusion = f32[64,1,128]{2,1,0:T(1,128)S(1)} fusion(f32[64,128,1]{1,2,0:T(1,128)S(1)} %bitcast.283, f32[1,64,128,128]{3,2,1,0:T(8,128)} %param.23), kind=kOutput, calls=%fused_computation.4 | convolution fusion | flops 12582912 | bytes 4259840 | tf_op jit(solution)/shard_map/bji,bj->bi/dot_general | solution.py:118
  244.9 8.0 %scatter_fusion = f32[16,8,128]{2,1,0:T(8,128)} fusion(f32[16,8,128]{2,1,0:T(8,128)} %broadcast_in_dim.30, s32[64]{0:T(128)S(1)} %get-tuple-element.128, f32[64,128]{1,0:T(8,128)S(1)} %broadcast_multiply_fusion), kind=kCustom, calls=%fused_computation.2 | custom fusion | flops 8192 | bytes 98816 | tf_op jit(solution)/shard_map/scatter-add | solution.py:123
  252.9 4.8 %all-to-all-start.1 = ((f32[16,8,128]{2,1,0:T(8,128)}), f32[16,8,128]{2,1,0:T(8,128)S(1)}, u32[]{:S(2)}, u32[]{:S(2)}) async-start(f32[16,8,128]{2,1,0:T(8,128)} %scatter_fusion), calls=%async_computation.1 | async-start | bytes 131072 | tf_op jit(solution)/shard_map/all_to_all | solution.py:125
  257.9 5.9 %all-to-all-done.1 = f32[16,8,128]{2,1,0:T(8,128)S(1)} async-done(((f32[16,8,128]{2,1,0:T(8,128)}), f32[16,8,128]{2,1,0:T(8,128)S(1)}, u32[]{:S(2)}, u32[]{:S(2)}) %all-to-all-start.1) | async-done | bytes 65568 | tf_op jit(solution)/shard_map/all_to_all | solution.py:125
  265.0 4.1 %copy.142 = f32[1,128,8,512]{3,2,1,0:T(8,128)} copy(f32[1,128,8,512]{3,1,2,0:T(8,128)} %copy-done.8) | data formatting | bytes 4194304
  272.9 3.0 multiply_multiply_fusion
  276.8 3.2 collective-permute-start.26
  280.0 2.7 collective-permute-start.27
  286.8 4.9 %copy_multiply_fusion.2 = (f32[1,128,8,512]{3,1,2,0:T(8,128)S(1)}, f32[1,128,8,512]{3,1,2,0:T(8,128)S(1)}) fusion(f32[1,128,8,512]{3,2,1,0:T(8,128)S(1)} %copy-done.1, f32[1,128,128]{2,1,0:T(8,128)S(1)} %copy-done, f32[1,128,8,512]{3,1,2,0:T(8,128)S(1)} %copy-done.6, f32[8,512]{1,0:T(8,128)S(1)} %convert_select_fusion, ...), kind=kOutput, calls=%fused_computation.198 | convolution fusion | flops 813170688 | bytes 15286272 | tf_op jit(solution)/shard_map/clm,cmrx->clrx/dot_general | solution.py:36
  294.4 4.4 %collective-permute-start.29 = (f32[1,128,1,512]{3,1,2,0:T(8,128)S(1)}, f32[1,128,1,512]{3,1,2,0:T(8,128)S(1)}, u32[]{:S(2)}, u32[]{:S(2)}) collective-permute-start(f32[1,128,1,512]{3,1,2,0:T(8,128)S(1)} %get-tuple-element.49), channel_id=1, source_target_pairs={{0,1},{1,2},{2,3},{3,4},{4,5},{5,6},{6,7},{7,8},{8,9},{9,10},{10,1... | collective-permute-start | bytes 786440 | tf_op jit(solution)/shard_map/ppermute | solution.py:25
  303.0 4.7 %copy_multiply_fusion.1 = (f32[1,128,8,512]{3,1,2,0:T(8,128)S(1)}, f32[1,128,8,512]{3,1,2,0:T(8,128)S(1)}) fusion(f32[1,128,8,512]{3,2,1,0:T(8,128)S(1)} %copy-done.1, f32[1,128,128]{2,1,0:T(8,128)S(1)} %copy-done, f32[1,128,8,512]{3,1,2,0:T(8,128)S(1)} %get-tuple-element.139, f32[1,128,8,512]{3,1,2,0:T(8,128)S(1)} %get-tuple-element.138, ...), kind=kOutput, calls=%fused_computation.197 | convolution fusion | flops 812122112 | bytes 15286272 | tf_op jit(solution)/shard_map/clm,cmrx->clrx/dot_general | solution.py:36
  310.5 4.6 %collective-permute-start.31 = (f32[1,128,1,512]{3,1,2,0:T(8,128)S(1)}, f32[1,128,1,512]{3,1,2,0:T(8,128)S(1)}, u32[]{:S(2)}, u32[]{:S(2)}) collective-permute-start(f32[1,128,1,512]{3,1,2,0:T(8,128)S(1)} %get-tuple-element.43), channel_id=1, source_target_pairs={{0,1},{1,2},{2,3},{3,4},{4,5},{5,6},{6,7},{7,8},{8,9},{9,10},{10,1... | collective-permute-start | bytes 786440 | tf_op jit(solution)/shard_map/ppermute | solution.py:25
  319.1 4.7 %copy_multiply_fusion = (f32[1,128,8,512]{3,1,2,0:T(8,128)S(1)}, f32[1,128,8,512]{3,1,2,0:T(8,128)S(1)}) fusion(f32[1,128,8,512]{3,2,1,0:T(8,128)S(1)} %copy-done.1, f32[1,128,128]{2,1,0:T(8,128)S(1)} %copy-done, f32[1,128,8,512]{3,1,2,0:T(8,128)S(1)} %get-tuple-element.141, f32[1,128,8,512]{3,1,2,0:T(8,128)S(1)} %get-tuple-element.140, ...), kind=kOutput, calls=%fused_computation.196 | convolution fusion | flops 812122112 | bytes 15286272 | tf_op jit(solution)/shard_map/clm,cmrx->clrx/dot_general | solution.py:36
  326.8 4.4 %collective-permute-start.33 = (f32[1,128,1,512]{3,1,2,0:T(8,128)S(1)}, f32[1,128,1,512]{3,1,2,0:T(8,128)S(1)}, u32[]{:S(2)}, u32[]{:S(2)}) collective-permute-start(f32[1,128,1,512]{3,1,2,0:T(8,128)S(1)} %get-tuple-element.37), channel_id=1, source_target_pairs={{0,1},{1,2},{2,3},{3,4},{4,5},{5,6},{6,7},{7,8},{8,9},{9,10},{10,1... | collective-permute-start | bytes 786440 | tf_op jit(solution)/shard_map/ppermute | solution.py:25
  335.4 4.7 %fusion.7 = f32[1,128,8,512]{3,1,2,0:T(8,128)S(1)} fusion(f32[1,128,8,512]{3,1,2,0:T(8,128)S(1)} %get-tuple-element.142, f32[1,128,1,512]{3,1,2,0:T(8,128)S(1)} %collective-permute-done.33, f32[1,128,8,512]{3,1,2,0:T(8,128)S(1)} %get-tuple-element.143, f32[1,128,1,512]{3,1,2,0:T(8,128)S(1)} %collective-permute-done.32, ...), kind=kOutput, calls=%fused_computation.12 | convolution fusion | flops 811597824 | bytes 13172736 | tf_op jit(solution)/shard_map/clm,cmrx->clrx/dot_general | solution.py:36
  (165 shorter events, 115.3 us)
Async XLA Ops:
  0.6 14.5 %copy-start = (f32[1,128,128]{2,1,0:T(8,128)S(1)}, f32[1,128,128]{2,1,0:T(8,128)}, u32[]{:S(2)}) copy-start(f32[1,128,128]{2,1,0:T(8,128)} %param.17) | copy-start | bytes 196612
  3.5 6.5 %copy-start.4 = (f32[1,128,8,512]{3,1,2,0:T(8,128)}, f32[1,128,8,512]{3,1,2,0:T(8,128)S(1)}, u32[]{:S(2)}) copy-start(f32[1,128,8,512]{3,1,2,0:T(8,128)S(1)} %copy.88) | copy-start | bytes 6291460
  3.5 11.4 %collective-permute-start = (f32[1,128,1,512]{3,1,2,0:T(8,128)S(1)}, f32[1,128,1,512]{3,1,2,0:T(8,128)S(1)}, u32[]{:S(2)}, u32[]{:S(2)}) collective-permute-start(f32[1,128,1,512]{3,1,2,0:T(8,128)S(1)} %get-tuple-element.126), channel_id=1, source_target_pairs={{1,0},{2,1},{3,2},{4,3},{5,4},{6,5},{7,6},{8,7},{9,8},{10,9},{11,1... | collective-permute-start | bytes 786440 | tf_op jit(solution)/shard_map/ppermute | solution.py:26
  5.5 9.6 %collective-permute-start.1 = (f32[1,128,1,512]{3,1,2,0:T(8,128)S(1)}, f32[1,128,1,512]{3,1,2,0:T(8,128)S(1)}, u32[]{:S(2)}, u32[]{:S(2)}) collective-permute-start(f32[1,128,1,512]{3,1,2,0:T(8,128)S(1)} %get-tuple-element.127), channel_id=1, source_target_pairs={{0,1},{1,2},{2,3},{3,4},{4,5},{5,6},{6,7},{7,8},{8,9},{9,10},{10,1... | collective-permute-start | bytes 786440 | tf_op jit(solution)/shard_map/ppermute | solution.py:25
  10.0 2.8 copy-start.11
  10.0 2.9 copy-start.12
  10.0 3.5 %copy-start.10 = (s32[8,512]{1,0:T(8,128)S(1)}, s32[8,512]{1,0:T(8,128)}, u32[]{:S(2)}) copy-start(s32[8,512]{1,0:T(8,128)} %param.18) | copy-start | bytes 49156
  25.9 8.4 %collective-permute-start.2 = (f32[1,128,1,512]{3,1,2,0:T(8,128)S(1)}, f32[1,128,1,512]{3,1,2,0:T(8,128)S(1)}, u32[]{:S(2)}, u32[]{:S(2)}) collective-permute-start(f32[1,128,1,512]{3,1,2,0:T(8,128)S(1)} %get-tuple-element.120), channel_id=1, source_target_pairs={{1,0},{2,1},{3,2},{4,3},{5,4},{6,5},{7,6},{8,7},{9,8},{10,9},{11,1... | collective-permute-start | bytes 786440 | tf_op jit(solution)/shard_map/ppermute | solution.py:26
  27.8 9.6 %collective-permute-start.3 = (f32[1,128,1,512]{3,1,2,0:T(8,128)S(1)}, f32[1,128,1,512]{3,1,2,0:T(8,128)S(1)}, u32[]{:S(2)}, u32[]{:S(2)}) collective-permute-start(f32[1,128,1,512]{3,1,2,0:T(8,128)S(1)} %get-tuple-element.121), channel_id=1, source_target_pairs={{0,1},{1,2},{2,3},{3,4},{4,5},{5,6},{6,7},{7,8},{8,9},{9,10},{10,1... | collective-permute-start | bytes 786440 | tf_op jit(solution)/shard_map/ppermute | solution.py:25
  42.8 8.4 %collective-permute-start.4 = (f32[1,128,1,512]{3,1,2,0:T(8,128)S(1)}, f32[1,128,1,512]{3,1,2,0:T(8,128)S(1)}, u32[]{:S(2)}, u32[]{:S(2)}) collective-permute-start(f32[1,128,1,512]{3,1,2,0:T(8,128)S(1)} %get-tuple-element.114), channel_id=1, source_target_pairs={{1,0},{2,1},{3,2},{4,3},{5,4},{6,5},{7,6},{8,7},{9,8},{10,9},{11,1... | collective-permute-start | bytes 786440 | tf_op jit(solution)/shard_map/ppermute | solution.py:26
  44.7 8.6 %collective-permute-start.5 = (f32[1,128,1,512]{3,1,2,0:T(8,128)S(1)}, f32[1,128,1,512]{3,1,2,0:T(8,128)S(1)}, u32[]{:S(2)}, u32[]{:S(2)}) collective-permute-start(f32[1,128,1,512]{3,1,2,0:T(8,128)S(1)} %get-tuple-element.115), channel_id=1, source_target_pairs={{0,1},{1,2},{2,3},{3,4},{4,5},{5,6},{6,7},{7,8},{8,9},{9,10},{10,1... | collective-permute-start | bytes 786440 | tf_op jit(solution)/shard_map/ppermute | solution.py:25
  58.8 8.4 %collective-permute-start.6 = (f32[1,128,1,512]{3,1,2,0:T(8,128)S(1)}, f32[1,128,1,512]{3,1,2,0:T(8,128)S(1)}, u32[]{:S(2)}, u32[]{:S(2)}) collective-permute-start(f32[1,128,1,512]{3,1,2,0:T(8,128)S(1)} %get-tuple-element.108), channel_id=1, source_target_pairs={{1,0},{2,1},{3,2},{4,3},{5,4},{6,5},{7,6},{8,7},{9,8},{10,9},{11,1... | collective-permute-start | bytes 786440 | tf_op jit(solution)/shard_map/ppermute | solution.py:26
  60.7 8.7 %collective-permute-start.7 = (f32[1,128,1,512]{3,1,2,0:T(8,128)S(1)}, f32[1,128,1,512]{3,1,2,0:T(8,128)S(1)}, u32[]{:S(2)}, u32[]{:S(2)}) collective-permute-start(f32[1,128,1,512]{3,1,2,0:T(8,128)S(1)} %get-tuple-element.109), channel_id=1, source_target_pairs={{0,1},{1,2},{2,3},{3,4},{4,5},{5,6},{6,7},{7,8},{8,9},{9,10},{10,1... | collective-permute-start | bytes 786440 | tf_op jit(solution)/shard_map/ppermute | solution.py:25
  69.4 8.0 %copy-start.13 = (s32[1,1,8]{2,1,0:T(1,128)S(1)}, s32[1,1,8]{2,1,0:T(1,128)}, u32[]{:S(2)}) copy-start(s32[1,1,8]{2,1,0:T(1,128)} %param.22) | copy-start | bytes 100
  76.1 3.3 collective-permute-start.8
  79.3 13.3 %all-to-all-start = ((f32[16,8,128]{2,1,0:T(8,128)}), f32[16,8,128]{2,1,0:T(8,128)S(1)}, u32[]{:S(2)}, u32[]{:S(2)}) async-start(f32[16,8,128]{2,1,0:T(8,128)} %collective-permute-done.8), calls=%async_computation | async-start | bytes 131072 | tf_op jit(solution)/shard_map/all_to_all | solution.py:104
  93.2 8.3 %copy-start.14 = (s32[1,1,64]{2,1,0:T(1,128)S(1)}, s32[1,1,64]{2,1,0:T(1,128)}, u32[]{:S(2)}) copy-start(s32[1,1,64]{2,1,0:T(1,128)} %param.21) | copy-start | bytes 772
  103.5 3.1 copy-start.3
  106.7 5.9 %collective-permute-start.10 = (f32[1,128,1,512]{3,1,2,0:T(8,128)S(1)}, f32[1,128,1,512]{3,1,2,0:T(8,128)S(1)}, u32[]{:S(2)}, u32[]{:S(2)}) collective-permute-start(f32[1,128,1,512]{3,1,2,0:T(8,128)S(1)} %get-tuple-element.103), channel_id=1, source_target_pairs={{0,1},{1,2},{2,3},{3,4},{4,5},{5,6},{6,7},{7,8},{8,9},{9,10},{10,1... | collective-permute-start | bytes 786440 | tf_op jit(solution)/shard_map/ppermute | solution.py:25
  109.3 7.7 %collective-permute-start.9 = (f32[1,128,1,512]{3,1,2,0:T(8,128)S(1)}, f32[1,128,1,512]{3,1,2,0:T(8,128)S(1)}, u32[]{:S(2)}, u32[]{:S(2)}) collective-permute-start(f32[1,128,1,512]{3,1,2,0:T(8,128)S(1)} %get-tuple-element.102), channel_id=1, source_target_pairs={{1,0},{2,1},{3,2},{4,3},{5,4},{6,5},{7,6},{8,7},{9,8},{10,9},{11,1... | collective-permute-start | bytes 786440 | tf_op jit(solution)/shard_map/ppermute | solution.py:26
  122.4 7.7 %collective-permute-start.11 = (f32[1,128,1,512]{3,1,2,0:T(8,128)S(1)}, f32[1,128,1,512]{3,1,2,0:T(8,128)S(1)}, u32[]{:S(2)}, u32[]{:S(2)}) collective-permute-start(f32[1,128,1,512]{3,1,2,0:T(8,128)S(1)} %get-tuple-element.96), channel_id=1, source_target_pairs={{1,0},{2,1},{3,2},{4,3},{5,4},{6,5},{7,6},{8,7},{9,8},{10,9},{11,1... | collective-permute-start | bytes 786440 | tf_op jit(solution)/shard_map/ppermute | solution.py:26
  124.3 9.6 %collective-permute-start.12 = (f32[1,128,1,512]{3,1,2,0:T(8,128)S(1)}, f32[1,128,1,512]{3,1,2,0:T(8,128)S(1)}, u32[]{:S(2)}, u32[]{:S(2)}) collective-permute-start(f32[1,128,1,512]{3,1,2,0:T(8,128)S(1)} %get-tuple-element.97), channel_id=1, source_target_pairs={{0,1},{1,2},{2,3},{3,4},{4,5},{5,6},{6,7},{7,8},{8,9},{9,10},{10,1... | collective-permute-start | bytes 786440 | tf_op jit(solution)/shard_map/ppermute | solution.py:25
  139.4 8.4 %collective-permute-start.13 = (f32[1,128,1,512]{3,1,2,0:T(8,128)S(1)}, f32[1,128,1,512]{3,1,2,0:T(8,128)S(1)}, u32[]{:S(2)}, u32[]{:S(2)}) collective-permute-start(f32[1,128,1,512]{3,1,2,0:T(8,128)S(1)} %get-tuple-element.90), channel_id=1, source_target_pairs={{1,0},{2,1},{3,2},{4,3},{5,4},{6,5},{7,6},{8,7},{9,8},{10,9},{11,1... | collective-permute-start | bytes 786440 | tf_op jit(solution)/shard_map/ppermute | solution.py:26
  141.3 8.6 %collective-permute-start.14 = (f32[1,128,1,512]{3,1,2,0:T(8,128)S(1)}, f32[1,128,1,512]{3,1,2,0:T(8,128)S(1)}, u32[]{:S(2)}, u32[]{:S(2)}) collective-permute-start(f32[1,128,1,512]{3,1,2,0:T(8,128)S(1)} %get-tuple-element.91), channel_id=1, source_target_pairs={{0,1},{1,2},{2,3},{3,4},{4,5},{5,6},{6,7},{7,8},{8,9},{9,10},{10,1... | collective-permute-start | bytes 786440 | tf_op jit(solution)/shard_map/ppermute | solution.py:25
  155.2 10.7 %copy-start.9 = (f32[1,128,8,512]{3,2,1,0:T(8,128)S(1)}, f32[1,128,8,512]{3,2,1,0:T(8,128)}, u32[]{:S(2)}) copy-start(f32[1,128,8,512]{3,2,1,0:T(8,128)} %param.15) | copy-start | bytes 6291460
  155.3 8.6 %collective-permute-start.15 = (f32[1,128,1,512]{3,1,2,0:T(8,128)S(1)}, f32[1,128,1,512]{3,1,2,0:T(8,128)S(1)}, u32[]{:S(2)}, u32[]{:S(2)}) collective-permute-start(f32[1,128,1,512]{3,1,2,0:T(8,128)S(1)} %get-tuple-element.84), channel_id=1, source_target_pairs={{1,0},{2,1},{3,2},{4,3},{5,4},{6,5},{7,6},{8,7},{9,8},{10,9},{11,1... | collective-permute-start | bytes 786440 | tf_op jit(solution)/shard_map/ppermute | solution.py:26
  157.4 8.6 %collective-permute-start.16 = (f32[1,128,1,512]{3,1,2,0:T(8,128)S(1)}, f32[1,128,1,512]{3,1,2,0:T(8,128)S(1)}, u32[]{:S(2)}, u32[]{:S(2)}) collective-permute-start(f32[1,128,1,512]{3,1,2,0:T(8,128)S(1)} %get-tuple-element.85), channel_id=1, source_target_pairs={{0,1},{1,2},{2,3},{3,4},{4,5},{5,6},{6,7},{7,8},{8,9},{9,10},{10,1... | collective-permute-start | bytes 786440 | tf_op jit(solution)/shard_map/ppermute | solution.py:25
  171.5 11.4 %copy-start.8 = (f32[1,128,8,512]{3,1,2,0:T(8,128)}, f32[1,128,8,512]{3,1,2,0:T(8,128)S(1)}, u32[]{:S(2)}) copy-start(f32[1,128,8,512]{3,1,2,0:T(8,128)S(1)} %get-tuple-element.131) | copy-start | bytes 6291460
  172.4 8.4 %collective-permute-start.17 = (f32[1,128,1,512]{3,1,2,0:T(8,128)S(1)}, f32[1,128,1,512]{3,1,2,0:T(8,128)S(1)}, u32[]{:S(2)}, u32[]{:S(2)}) collective-permute-start(f32[1,128,1,512]{3,1,2,0:T(8,128)S(1)} %get-tuple-element.78), channel_id=1, source_target_pairs={{1,0},{2,1},{3,2},{4,3},{5,4},{6,5},{7,6},{8,7},{9,8},{10,9},{11,1... | collective-permute-start | bytes 786440 | tf_op jit(solution)/shard_map/ppermute | solution.py:26
  174.5 8.4 %collective-permute-start.18 = (f32[1,128,1,512]{3,1,2,0:T(8,128)S(1)}, f32[1,128,1,512]{3,1,2,0:T(8,128)S(1)}, u32[]{:S(2)}, u32[]{:S(2)}) collective-permute-start(f32[1,128,1,512]{3,1,2,0:T(8,128)S(1)} %get-tuple-element.79), channel_id=1, source_target_pairs={{0,1},{1,2},{2,3},{3,4},{4,5},{5,6},{6,7},{7,8},{8,9},{9,10},{10,1... | collective-permute-start | bytes 786440 | tf_op jit(solution)/shard_map/ppermute | solution.py:25
  190.7 8.4 %collective-permute-start.19 = (f32[1,128,1,512]{3,1,2,0:T(8,128)S(1)}, f32[1,128,1,512]{3,1,2,0:T(8,128)S(1)}, u32[]{:S(2)}, u32[]{:S(2)}) collective-permute-start(f32[1,128,1,512]{3,1,2,0:T(8,128)S(1)} %get-tuple-element.72), channel_id=1, source_target_pairs={{1,0},{2,1},{3,2},{4,3},{5,4},{6,5},{7,6},{8,7},{9,8},{10,9},{11,1... | collective-permute-start | bytes 786440 | tf_op jit(solution)/shard_map/ppermute | solution.py:26
  192.7 8.8 %collective-permute-start.20 = (f32[1,128,1,512]{3,1,2,0:T(8,128)S(1)}, f32[1,128,1,512]{3,1,2,0:T(8,128)S(1)}, u32[]{:S(2)}, u32[]{:S(2)}) collective-permute-start(f32[1,128,1,512]{3,1,2,0:T(8,128)S(1)} %get-tuple-element.73), channel_id=1, source_target_pairs={{0,1},{1,2},{2,3},{3,4},{4,5},{5,6},{6,7},{7,8},{8,9},{9,10},{10,1... | collective-permute-start | bytes 786440 | tf_op jit(solution)/shard_map/ppermute | solution.py:25
  207.0 8.4 %collective-permute-start.21 = (f32[1,128,1,512]{3,1,2,0:T(8,128)S(1)}, f32[1,128,1,512]{3,1,2,0:T(8,128)S(1)}, u32[]{:S(2)}, u32[]{:S(2)}) collective-permute-start(f32[1,128,1,512]{3,1,2,0:T(8,128)S(1)} %get-tuple-element.66), channel_id=1, source_target_pairs={{1,0},{2,1},{3,2},{4,3},{5,4},{6,5},{7,6},{8,7},{9,8},{10,9},{11,1... | collective-permute-start | bytes 786440 | tf_op jit(solution)/shard_map/ppermute | solution.py:26
  208.9 8.6 %collective-permute-start.22 = (f32[1,128,1,512]{3,1,2,0:T(8,128)S(1)}, f32[1,128,1,512]{3,1,2,0:T(8,128)S(1)}, u32[]{:S(2)}, u32[]{:S(2)}) collective-permute-start(f32[1,128,1,512]{3,1,2,0:T(8,128)S(1)} %get-tuple-element.67), channel_id=1, source_target_pairs={{0,1},{1,2},{2,3},{3,4},{4,5},{5,6},{6,7},{7,8},{8,9},{9,10},{10,1... | collective-permute-start | bytes 786440 | tf_op jit(solution)/shard_map/ppermute | solution.py:25
  223.1 8.4 %collective-permute-start.23 = (f32[1,128,1,512]{3,1,2,0:T(8,128)S(1)}, f32[1,128,1,512]{3,1,2,0:T(8,128)S(1)}, u32[]{:S(2)}, u32[]{:S(2)}) collective-permute-start(f32[1,128,1,512]{3,1,2,0:T(8,128)S(1)} %get-tuple-element.60), channel_id=1, source_target_pairs={{1,0},{2,1},{3,2},{4,3},{5,4},{6,5},{7,6},{8,7},{9,8},{10,9},{11,1... | collective-permute-start | bytes 786440 | tf_op jit(solution)/shard_map/ppermute | solution.py:26
  225.1 8.6 %collective-permute-start.24 = (f32[1,128,1,512]{3,1,2,0:T(8,128)S(1)}, f32[1,128,1,512]{3,1,2,0:T(8,128)S(1)}, u32[]{:S(2)}, u32[]{:S(2)}) collective-permute-start(f32[1,128,1,512]{3,1,2,0:T(8,128)S(1)} %get-tuple-element.61), channel_id=1, source_target_pairs={{0,1},{1,2},{2,3},{3,4},{4,5},{5,6},{6,7},{7,8},{8,9},{9,10},{10,1... | collective-permute-start | bytes 786440 | tf_op jit(solution)/shard_map/ppermute | solution.py:25
  252.9 10.8 %all-to-all-start.1 = ((f32[16,8,128]{2,1,0:T(8,128)}), f32[16,8,128]{2,1,0:T(8,128)S(1)}, u32[]{:S(2)}, u32[]{:S(2)}) async-start(f32[16,8,128]{2,1,0:T(8,128)} %scatter_fusion), calls=%async_computation.1 | async-start | bytes 131072 | tf_op jit(solution)/shard_map/all_to_all | solution.py:125
  263.7 5.4 %collective-permute-start.25 = (f32[16,8,128]{2,1,0:T(8,128)S(1)}, f32[16,8,128]{2,1,0:T(8,128)S(1)}, u32[]{:S(2)}, u32[]{:S(2)}) collective-permute-start(f32[16,8,128]{2,1,0:T(8,128)S(1)} %all-to-all-done.1), channel_id=1, source_target_pairs={{0,16},{16,0},{1,17},{17,1},{2,18},{18,2},{3,19},{19,3},{4,20},{20... | collective-permute-start | bytes 196616 | tf_op jit(solution)/shard_map/ppermute | solution.py:15
  276.7 10.1 %copy-start.6 = (f32[1,128,8,512]{3,1,2,0:T(8,128)S(1)}, f32[1,128,8,512]{3,1,2,0:T(8,128)}, u32[]{:S(2)}) copy-start(f32[1,128,8,512]{3,1,2,0:T(8,128)} %scatter-add.27) | copy-start | bytes 6291460
  276.8 7.8 %collective-permute-start.26 = (f32[1,128,1,512]{3,1,2,0:T(8,128)S(1)}, f32[1,128,1,512]{3,1,2,0:T(8,128)S(1)}, u32[]{:S(2)}, u32[]{:S(2)}) collective-permute-start(f32[1,128,1,512]{3,1,2,0:T(8,128)S(1)} %get-tuple-element.54), channel_id=1, source_target_pairs={{1,0},{2,1},{3,2},{4,3},{5,4},{6,5},{7,6},{8,7},{9,8},{10,9},{11,1... | collective-permute-start | bytes 786440 | tf_op jit(solution)/shard_map/ppermute | solution.py:26
  280.0 6.8 %collective-permute-start.27 = (f32[1,128,1,512]{3,1,2,0:T(8,128)S(1)}, f32[1,128,1,512]{3,1,2,0:T(8,128)S(1)}, u32[]{:S(2)}, u32[]{:S(2)}) collective-permute-start(f32[1,128,1,512]{3,1,2,0:T(8,128)S(1)} %get-tuple-element.55), channel_id=1, source_target_pairs={{0,1},{1,2},{2,3},{3,4},{4,5},{5,6},{6,7},{7,8},{8,9},{9,10},{10,1... | collective-permute-start | bytes 786440 | tf_op jit(solution)/shard_map/ppermute | solution.py:25
  292.5 8.4 %collective-permute-start.28 = (f32[1,128,1,512]{3,1,2,0:T(8,128)S(1)}, f32[1,128,1,512]{3,1,2,0:T(8,128)S(1)}, u32[]{:S(2)}, u32[]{:S(2)}) collective-permute-start(f32[1,128,1,512]{3,1,2,0:T(8,128)S(1)} %get-tuple-element.48), channel_id=1, source_target_pairs={{1,0},{2,1},{3,2},{4,3},{5,4},{6,5},{7,6},{8,7},{9,8},{10,9},{11,1... | collective-permute-start | bytes 786440 | tf_op jit(solution)/shard_map/ppermute | solution.py:26
  294.4 8.6 %collective-permute-start.29 = (f32[1,128,1,512]{3,1,2,0:T(8,128)S(1)}, f32[1,128,1,512]{3,1,2,0:T(8,128)S(1)}, u32[]{:S(2)}, u32[]{:S(2)}) collective-permute-start(f32[1,128,1,512]{3,1,2,0:T(8,128)S(1)} %get-tuple-element.49), channel_id=1, source_target_pairs={{0,1},{1,2},{2,3},{3,4},{4,5},{5,6},{6,7},{7,8},{8,9},{9,10},{10,1... | collective-permute-start | bytes 786440 | tf_op jit(solution)/shard_map/ppermute | solution.py:25
  308.6 8.4 %collective-permute-start.30 = (f32[1,128,1,512]{3,1,2,0:T(8,128)S(1)}, f32[1,128,1,512]{3,1,2,0:T(8,128)S(1)}, u32[]{:S(2)}, u32[]{:S(2)}) collective-permute-start(f32[1,128,1,512]{3,1,2,0:T(8,128)S(1)} %get-tuple-element.42), channel_id=1, source_target_pairs={{1,0},{2,1},{3,2},{4,3},{5,4},{6,5},{7,6},{8,7},{9,8},{10,9},{11,1... | collective-permute-start | bytes 786440 | tf_op jit(solution)/shard_map/ppermute | solution.py:26
  310.5 8.6 %collective-permute-start.31 = (f32[1,128,1,512]{3,1,2,0:T(8,128)S(1)}, f32[1,128,1,512]{3,1,2,0:T(8,128)S(1)}, u32[]{:S(2)}, u32[]{:S(2)}) collective-permute-start(f32[1,128,1,512]{3,1,2,0:T(8,128)S(1)} %get-tuple-element.43), channel_id=1, source_target_pairs={{0,1},{1,2},{2,3},{3,4},{4,5},{5,6},{6,7},{7,8},{8,9},{9,10},{10,1... | collective-permute-start | bytes 786440 | tf_op jit(solution)/shard_map/ppermute | solution.py:25
  324.7 10.7 %copy-start.7 = (f32[1,128,8,512]{3,2,1,0:T(8,128)S(1)}, f32[1,128,8,512]{3,2,1,0:T(8,128)}, u32[]{:S(2)}) copy-start(f32[1,128,8,512]{3,2,1,0:T(8,128)} %param.14) | copy-start | bytes 6291460
  324.7 8.6 %collective-permute-start.32 = (f32[1,128,1,512]{3,1,2,0:T(8,128)S(1)}, f32[1,128,1,512]{3,1,2,0:T(8,128)S(1)}, u32[]{:S(2)}, u32[]{:S(2)}) collective-permute-start(f32[1,128,1,512]{3,1,2,0:T(8,128)S(1)} %get-tuple-element.36), channel_id=1, source_target_pairs={{1,0},{2,1},{3,2},{4,3},{5,4},{6,5},{7,6},{8,7},{9,8},{10,9},{11,1... | collective-permute-start | bytes 786440 | tf_op jit(solution)/shard_map/ppermute | solution.py:26
  326.8 8.6 %collective-permute-start.33 = (f32[1,128,1,512]{3,1,2,0:T(8,128)S(1)}, f32[1,128,1,512]{3,1,2,0:T(8,128)S(1)}, u32[]{:S(2)}, u32[]{:S(2)}) collective-permute-start(f32[1,128,1,512]{3,1,2,0:T(8,128)S(1)} %get-tuple-element.37), channel_id=1, source_target_pairs={{0,1},{1,2},{2,3},{3,4},{4,5},{5,6},{6,7},{7,8},{8,9},{9,10},{10,1... | collective-permute-start | bytes 786440 | tf_op jit(solution)/shard_map/ppermute | solution.py:25
  (3 other events, 4.9 us)
where the time goes:
time: 350 us; the launch traced here: 343 us
  starting transfers between devices  115 us (33%)
  matrix products  96.4 us (28%)
  waiting for transfers between devices  76.2 us (22%)
  local copies, waits for them, and re-layouts  40.1 us (11%)
  other arithmetic  13.4 us (4%)
    dot_general x16, matrix products, column_mix(): jnp.einsum('clm,cmrx->clrx', matrix, system_variables, precision=precise)  82.3 us
    ppermute x16, starting transfers between devices, with_halo(): before = lax.ppermute(last, axis, up)  67.5 us
    ppermute x16, waiting for transfers between devices, with_halo(): before = lax.ppermute(last, axis, up)  33.2 us
    ppermute x16, starting transfers between devices, with_halo(): after = lax.ppermute(first, axis, down)  32.9 us
    ppermute x16, waiting for transfers between devices, with_halo(): after = lax.ppermute(first, axis, down)  29.3 us
    slice x32, local copies, waits for them, and re-layouts, side_sum(): jnp.roll(interior, 1, axis=3)  21.2 us
    unnamed x34, local copies, waits for them, and re-layouts  12.3 us
    dot_general x1, matrix products, shards(): jnp.einsum('bij,bj->bi', weights, picked, precision=precise) * live_mask  8.31 us
  transfers between devices with their start and end apart: 36, of which 34 were waited for; matrix products, arithmetic and copies ran while one was open for 4% of the time, Pallas kernels for 0%

commit v1 on v0

v1 whole, which is shorter than its diff:
```python
import functools

import jax
import jax.numpy as jnp
from jax import lax
from jax.experimental import pallas as pl
from jax.experimental.pallas import tpu as pltpu
from jax.sharding import PartitionSpec as P

STEPS = 4
CHUNKS = 2
SUB = 32
MESH = pl.DeviceIdType.MESH
precise = lax.Precision.HIGHEST
f32, bf16 = jnp.float32, jnp.bfloat16


def split(x):
    high = x.astype(bf16)
    return high, (x - high.astype(f32)).astype(bf16)


def mix(a_wide, a_low, x):
    high, low = split(x)
    both = jnp.concatenate([high, low], axis=0)
    return jnp.dot(a_wide, both, preferred_element_type=f32) + jnp.dot(
        a_low, high, preferred_element_type=f32
    )


def block(tiles, forward, backward, *refs):
    refs = list(refs)
    x_hbm, d_ref, a_ref, sea_ref = refs[:4]
    del refs[:4]
    add_ref = refs.pop(0)
    measured = refs.pop(0) if forward and backward else None
    outs = [refs.pop(0) for _ in range(bool(forward) + bool(backward))]
    state, halo, send_sem, recv_sem, io_sem, wide, low = refs[:7]
    del refs[:7]
    masked, wide_t, low_t = refs if backward else (None,) * 3
    comp, me = lax.axis_index("comp"), lax.axis_index("tile")
    rows, levels, lon = d_ref.shape
    width = lon // CHUNKS
    up, down = lax.rem(me + tiles - 1, tiles), lax.rem(me + 1, tiles)
    has_up, has_down = me > 0, me < tiles - 1
    has = (has_up, has_down)

    first = masked if not forward else state.at[0]
    load = pltpu.make_async_copy(x_hbm, first, io_sem.at[0])
    load.start()

    barrier = pltpu.get_barrier_semaphore()
    for there, other in ((has_up, up), (has_down, down)):

        @pl.when(there)
        def _():
            pl.semaphore_signal(barrier, inc=1, device_id=(comp, other), device_id_type=MESH)

    if forward:
        high, rest = split(a_ref[...])
        wide[...] = jnp.concatenate([high, high], axis=1)
        low[...] = rest
    if backward:
        high, rest = split(a_ref[...].T)
        wide_t[...] = jnp.concatenate([high, high], axis=1)
        low_t[...] = rest
    total = forward + backward
    for side in (0, 1):

        @pl.when(jnp.logical_not(has[side]))
        def _():
            def clear(i, _):
                halo[i, side] = jnp.zeros((levels, lon), f32)
                return _

            lax.fori_loop(0, total, clear, 0)

    pl.semaphore_wait(barrier, has_up.astype(jnp.int32) + has_down.astype(jnp.int32))
    load.wait()
    for r in range(rows):
        first[r, 0:1, :] = first[r, 0:1, :] + add_ref[r : r + 1, :]

    def copy(h, slot, side, c):
        columns = pl.ds(c * width, width)
        return pltpu.make_async_remote_copy(
            src_ref=state.at[slot, (rows - 1) * side, :, columns],
            dst_ref=halo.at[h, 1 - side, :, columns],
            send_sem=send_sem.at[h, side, c],
            recv_sem=recv_sem.at[h, 1 - side, c],
            device_id=(comp, (up, down)[side]),
            device_id_type=MESH,
        )

    def send(h, slot, side, c):
        @pl.when(has[side])
        def _():
            copy(h, slot, side, c).start()

    def receive(h, slot, side, c):
        @pl.when(has[side])
        def _():
            copy(h, slot, 1 - side, c).wait_recv()

    def pieces():
        return [slice(k, k + SUB) for k in range(0, levels, SUB)]

    def stencil(now, above, below, k, cols):
        x = now[k, :]
        left, right = pltpu.roll(x, 1, axis=1), pltpu.roll(x, lon - 1, axis=1)
        around = (left + right)[:, cols] + (above[k, cols] + below[k, cols])
        return x[:, cols], around - 4.0 * x[:, cols]

    def forward_row(slot, r, above, below, cols, target):
        now = state.at[slot, r]
        sea = sea_ref[pl.ds(r, 1), :][:, cols]
        y = mix(wide[...], low[...], now[:, cols])
        for k in pieces():
            x, lap = stencil(now, above, below, k, cols)
            target[r, k, cols] = sea * (x + d_ref[r, k, cols] * lap + y[k])

    def scaled_row(slot, r, cols, k, adjoint):
        u = sea_ref[pl.ds(r, 1), :][:, cols] * adjoint
        masked[r, k, cols] = u
        state[slot, r, k, cols] = d_ref[r, k, cols] * u

    def backward_row(slot, r, above, below, cols, last):
        now = state.at[slot, r]
        y = mix(wide_t[...], low_t[...], masked[r, :, cols])
        for k in pieces():
            _, lap = stencil(now, above, below, k, cols)
            adjoint = masked[r, k, cols] + lap + y[k]
            if last:
                masked[r, k, cols] = adjoint
            else:
                scaled_row(slot + 1, r, cols, k, adjoint)

    every = slice(0, lon)

    def step(h, slot, row, more):
        def inner(r, _):
            row(slot, r, state.at[slot, r - 1], state.at[slot, r + 1], every)
            return _

        lax.fori_loop(1, rows - 1, inner, 0)
        for c in range(CHUNKS):
            cols = slice(c * width, (c + 1) * width)
            for side in (0, 1):
                receive(h, slot, side, c)
                if side == 0:
                    row(slot, 0, halo.at[h, 0], state.at[slot, 1], cols)
                else:
                    row(slot, rows - 1, state.at[slot, rows - 2], halo.at[h, 1], cols)
                if more:
                    send(h + 1, slot + 1, side, c)

    def all_edges(h, slot):
        for c in range(CHUNKS):
            for side in (0, 1):
                send(h, slot, side, c)

    def run(base, slot0, count, make):
        def one(i, _):
            step(base + i, slot0 + i, make(False), True)
            return _

        lax.fori_loop(0, count - 1, one, 0)
        step(base + count - 1, slot0 + count - 1, make(True), False)

    base = 0
    slot0 = 0
    stores = []
    if forward:
        all_edges(0, 0)

        def make(last):
            return lambda slot, r, above, below, cols: forward_row(
                slot, r, above, below, cols, state.at[slot + 1]
            )

        run(0, 0, forward, make)
        base, slot0 = forward, forward + 1
        stores.append(pltpu.make_async_copy(state.at[forward], outs[0], io_sem.at[1]))
        stores[-1].start()
    if backward:

        def start_row(r, _):
            for k in pieces():
                if forward:
                    value = state[forward, r, k, :] - measured[r, k, :]
                else:
                    value = masked[r, k, :]
                scaled_row(slot0, r, every, k, value)
            return _

        start_row(0, 0)
        start_row(rows - 1, 0)
        all_edges(base, slot0)
        lax.fori_loop(1, rows - 1, start_row, 0)

        def make(last):
            return lambda slot, r, above, below, cols: backward_row(
                slot, r, above, below, cols, last
            )

        run(base, slot0, backward, make)
        stores.append(pltpu.make_async_copy(masked, outs[-1], io_sem.at[2]))
        stores[-1].start()
    for side in (0, 1):

        @pl.when(has[side])
        def _():
            for h in range(total):
                slot = h if h < forward else h + bool(forward)
                for c in range(CHUNKS):
                    copy(h, slot, side, c).wait_send()

    for store in stores:
        store.wait()


def run_block(tiles, ident, forward, backward, x, d, a, sea, add, measured=None):
    rows, levels, lon = x.shape
    total = forward + backward
    slots = (forward + 1 if forward else 0) + backward
    vmem = pl.BlockSpec(memory_space=pltpu.VMEM)
    hbm = pl.BlockSpec(memory_space=pl.ANY)
    operands = [x, d, a, sea, add] + ([measured] if measured is not None else [])
    outs = bool(forward) + bool(backward)
    scratch = [
        pltpu.VMEM((slots, rows, levels, lon), f32),
        pltpu.VMEM((total, 2, levels, lon), f32),
        pltpu.SemaphoreType.DMA((total, 2, CHUNKS)),
        pltpu.SemaphoreType.DMA((total, 2, CHUNKS)),
        pltpu.SemaphoreType.DMA((3,)),
        pltpu.VMEM((levels, 2 * levels), bf16),
        pltpu.VMEM((levels, levels), bf16),
    ]
    if backward:
        scratch += [
            pltpu.VMEM((rows, levels, lon), f32),
            pltpu.VMEM((levels, 2 * levels), bf16),
            pltpu.VMEM((levels, levels), bf16),
        ]
    return pl.pallas_call(
        functools.partial(block, tiles, forward, backward),
        out_shape=[jax.ShapeDtypeStruct(x.shape, f32)] * outs,
        in_specs=[hbm] + [vmem] * (len(operands) - 1),
        out_specs=[hbm] * outs,
        scratch_shapes=scratch,
        compiler_params=pltpu.CompilerParams(
            collective_id=ident, has_side_effects=True, vmem_limit_bytes=56 * 2**20
        ),
    )(*operands)


def swap_kernel(tiles, parcel, out, slots, send_sem, recv_sem):
    other, me = 1 - lax.axis_index("comp"), lax.axis_index("tile")
    barrier = pltpu.get_barrier_semaphore()
    for t in range(tiles):
        pl.semaphore_signal(barrier, inc=1, device_id=(other, t), device_id_type=MESH)
    pl.semaphore_wait(barrier, tiles)

    def copy(k, goes, lands):
        return pltpu.make_async_remote_copy(
            src_ref=parcel.at[goes],
            dst_ref=slots.at[lands],
            send_sem=send_sem.at[k],
            recv_sem=recv_sem.at[k],
            device_id=(other, goes),
            device_id_type=MESH,
        )

    for k in range(tiles):
        copy(k, lax.rem(me + k, tiles), me).start()
    for k in range(tiles):
        copy(k, lax.rem(me + k, tiles), lax.rem(me + tiles - k, tiles)).wait_recv()
    out[...] = slots[...]
    for k in range(tiles):
        copy(k, lax.rem(me + k, tiles), me).wait_send()


def swap(tiles, ident, parcel):
    vmem = pl.BlockSpec(memory_space=pltpu.VMEM)
    return pl.pallas_call(
        functools.partial(swap_kernel, tiles),
        out_shape=jax.ShapeDtypeStruct(parcel.shape, f32),
        in_specs=[vmem],
        out_specs=vmem,
        scratch_shapes=[
            pltpu.VMEM(parcel.shape, f32),
            pltpu.SemaphoreType.DMA((tiles,)),
            pltpu.SemaphoreType.DMA((tiles,)),
        ],
        compiler_params=pltpu.CompilerParams(collective_id=ident, has_side_effects=True),
    )(parcel)


def one_hot(index, count):
    return (index[:, None] == jnp.arange(count, dtype=jnp.int32)[None, :]).astype(f32)


def shards(
    starting_perturbation,
    measured_discrepancy,
    diffusion,
    vert_mix,
    ocean_mask,
    pair_tile,
    pair_patch,
    dest_patch,
    pair_blocks,
    remap_weight,
):
    component = lax.axis_index("comp")
    own_tile = lax.axis_index("tile")
    tiles = lax.axis_size("tile")
    row_count = starting_perturbation.shape[2]
    lon_count = starting_perturbation.shape[3]
    patch_len = remap_weight.shape[2]
    patch_count = row_count * lon_count // patch_len
    block_count = remap_weight.shape[1]
    pair_count = pair_tile.shape[2]
    per_pair = block_count // pair_count
    partner = 1 - component
    sea = jnp.where(component == 1, ocean_mask.astype(f32), 1.0)
    slot_ids = jnp.arange(block_count, dtype=jnp.int32) % per_pair
    own_tiles = jnp.repeat(pair_tile[component, own_tile], per_pair)
    live = (slot_ids < jnp.repeat(pair_blocks[0, 0], per_pair)).astype(f32)[:, None]
    landing = one_hot(dest_patch[0, 0], patch_count) * live
    weights = remap_weight[0]
    hits = (pair_tile[partner] == own_tile).astype(jnp.int32)
    feed = pair_patch[partner].reshape(tiles, pair_count, per_pair)
    send_rows = jnp.sum(hits[:, :, None] * feed, axis=1)
    sent = jnp.sum(hits, axis=1).astype(f32)
    sending = one_hot(send_rows.reshape(-1), patch_count) * jnp.repeat(sent, per_pair)[:, None]
    taking = one_hot(own_tiles * per_pair + slot_ids, tiles * per_pair)

    def to_rows(x):
        return jnp.swapaxes(x[0], 0, 1)

    start, measured, diff = map(
        to_rows, (starting_perturbation, measured_discrepancy, diffusion)
    )
    none = jnp.zeros((row_count, lon_count), f32)
    (middle,) = run_block(tiles, 0, STEPS, 0, start, diff, vert_mix[0], sea, none)

    surface = middle[:, 0].reshape(patch_count, patch_len)
    parcel = jnp.dot(sending, surface, precision=precise)
    arrived = swap(tiles, 1, parcel.reshape(tiles, per_pair, patch_len))
    picked = jnp.dot(taking, arrived.reshape(tiles * per_pair, patch_len), precision=precise)
    terms = jnp.sum(weights * picked[:, None, :], axis=2)
    summed = jnp.dot(landing.T, terms, precision=precise).reshape(row_count, lon_count)
    final, adjoint = run_block(
        tiles, 2, STEPS, STEPS, middle, diff, vert_mix[0], sea, sea * summed, measured
    )

    masked = sea.reshape(patch_count, patch_len) * adjoint[:, 0].reshape(patch_count, patch_len)
    spread = jnp.dot(landing, masked, precision=precise)
    terms = jnp.sum(weights * spread[:, :, None], axis=1)
    parcel = jnp.dot(taking.T, terms, precision=precise)
    back = swap(tiles, 3, parcel.reshape(tiles, per_pair, patch_len))
    returned = jnp.dot(sending.T, back.reshape(tiles * per_pair, patch_len), precision=precise)
    (last,) = run_block(
        tiles,
        4,
        0,
        STEPS,
        adjoint,
        diff,
        vert_mix[0],
        sea,
        returned.reshape(row_count, lon_count),
    )
    gradient = starting_perturbation + jnp.swapaxes(last, 0, 1)[None]
    return (jnp.swapaxes(final, 0, 1)[None], gradient)


def solution(mesh):
    placed = (
        P("comp", None, "tile", None),
        P("comp", None, "tile", None),
        P("comp", None, "tile", None),
        P("comp", None, None),
        P("tile", None),
        P(),
        P(),
        P("comp", "tile", None),
        P("comp", "tile", None),
        P("comp", "tile", None, None),
    )
    return jax.shard_map(
        shards,
        mesh=mesh,
        in_specs=placed,
        out_specs=(P("comp", None, "tile", None), P("comp", None, "tile", None)),
        check_vma=False,
    )
```

time: 350 us -> 181 us (0.52); the launches traced: 343 us -> 181 us
  Pallas kernels: 0 us -> 145 us
  starting transfers between devices: 115 us -> 0 us
  matrix products: 96.4 us -> 4.46 us
  waiting for transfers between devices: 76.2 us -> 0 us
  local copies, waits for them, and re-layouts: 40.1 us -> 18.1 us
    pallas_call x0 -> x5, Pallas kernels: none -> 145 us  [the longest x3 118 us: run_block(): pl.pallas_call(functools.partial(block, tiles, forward, backward), out_sh...]
    ppermute x34 -> x0, starting transfers between devices: 103 us -> none  [the longest x16 67.5 us: with_halo(): before = lax.ppermute(last, axis, up)]
    dot_general x19 -> x5, matrix products: 96.2 us -> 4.23 us  [the longest x1 1.14 us: shards(): jnp.dot(sending.T, back.reshape(tiles * per_pair, patch_len), precision=p...]
    ppermute x34 -> x0, waiting for transfers between devices: 64.3 us -> none  [the longest x16 33.2 us: with_halo(): before = lax.ppermute(last, axis, up)]
    slice x48 -> x2, local copies, waits for them, and re-layouts: 21.8 us -> 1.83 us  [the longest x1 0.91 us: shards(): surface = middle[:, 0].reshape(patch_count, patch_len)]
    all_to_all x2 -> x0, starting transfers between devices: 12 us -> none  [the longest x1 7.23 us: shards(): lax.all_to_all(crossed, 'tile', split_axis=0, concat_axis=0, tiled=True)]
    all_to_all x2 -> x0, waiting for transfers between devices: 11.9 us -> none  [the longest x1 6.02 us: shards(): lax.all_to_all(crossed, 'tile', split_axis=0, concat_axis=0, tiled=True)]
    scatter-add x2 -> x0, other arithmetic: 9.25 us -> none  [the longest x1 8 us: shards(): parcel = jnp.zeros((tile_count, per_pair, patch_len), jnp.float32).at[own...]
  transfers between devices with their start and end apart: 36 -> 0, of which waited for: 34 -> 0; matrix products, arithmetic and copies ran while one was open for 4% -> 0% of each run, Pallas kernels for 0% -> 0%
where the time goes in v1:
time: 181 us
  Pallas kernels  145 us (80%)
  local copies, waits for them, and re-layouts  18.1 us (10%)
  other arithmetic  12.2 us (7%)
  matrix products  4.46 us (2%)
    pallas_call x3, Pallas kernels, run_block(): pl.pallas_call(functools.partial(block, tiles, forward, backward), out_sh...  118 us
    pallas_call x2, Pallas kernels, swap(): pl.pallas_call(functools.partial(swap_kernel, tiles), out_shape=jax.Shape...  26.8 us
    unnamed x22, local copies, waits for them, and re-layouts  7.75 us
    transpose x1, local copies, waits for them, and re-layouts, to_rows(): return jnp.swapaxes(x[0], 0, 1)  6.66 us

profile of v1, /device:TPU:1, one launch (start us, length us, event | category | flops | bytes accessed | tf_op | source)
XLA Modules:
  0.0 180.7 jit_solution(4408473271086792338)
XLA Ops:
  0.6 0.0 copy-start
  0.7 0.7 convert_bitcast_fusion
  1.3 0.0 copy-done
  1.4 0.1 copy.35
  1.5 0.1 copy.29
  1.6 1.3 convert_select_fusion.refs_3_
  2.9 6.7 %copy_bitcast_fusion.1 = (f32[8,128,512]{2,1,0:T(8,128)}, f32[8,128,512]{2,1,0:T(8,128)}) fusion(f32[1,128,8,512]{3,2,1,0:T(8,128)} %param.12, f32[1,128,8,512]{3,2,1,0:T(8,128)} %param.10), kind=kLoop, calls=%fused_computation.6 | loop fusion | bytes 8388608 | tf_op jit(solution)/shard_map/transpose | solution.py:339
  9.5 0.6 broadcast_in_dim.31.refs_4_
  10.1 31.6 %shard_map.113.refs_0_ = f32[8,128,512]{2,1,0:T(8,128)} custom-call(f32[8,128,512]{2,1,0:T(8,128)} %get-tuple-element.15.refs_0_, f32[8,128,512]{2,1,0:T(8,128)} %get-tuple-element.14.refs_1_, f32[128,128]{1,0:T(8,128)} %bitcast.56, f32[8,512]{1,0:T(8,128)} %convert_select_fusion.refs_3_, f32[8,512]{1,0:T(8,128)} %broadcast_in_dim.31.refs_4_), custom_call_target="tpu_custom_call" | custom-call | tf_op jit(solution)/shard_map/pallas_call | solution.py:244
  41.8 0.9 slice.6
  42.7 0.9 fusion.6.parcel
  43.6 10.6 %shard_map.114 = f32[16,8,128]{2,1,0:T(8,128)} custom-call(f32[16,8,128]{2,1,0:T(8,128)} %fusion.6.parcel), custom_call_target="tpu_custom_call" | custom-call | tf_op jit(solution)/shard_map/pallas_call | solution.py:284
  54.2 0.0 copy-done.6
  54.2 0.2 multiply_reduce_fusion
  54.4 0.1 broadcast_in_dim.33
  54.5 0.1 mul.77
  54.6 1.1 fusion.4
  55.6 0.0 copy-start.7
  55.6 0.0 copy-start.8
  55.7 0.0 copy-start.5
  55.7 0.0 copy-start.2
  55.7 3.5 %fusion = f32[64,128]{1,0:T(8,128)S(1)} fusion(f32[1,64,128,128]{3,2,1,0:T(8,128)} %param.19, f32[64,128]{1,0:T(8,128)S(1)} %fusion.4), kind=kLoop, calls=%fused_computation.2 | loop fusion | flops 2088960 | bytes 4259840 | tf_op jit(solution)/shard_map/reduce_sum | solution.py:351
  59.2 0.0 copy-done.7
  59.2 0.1 broadcast_in_dim.32
  59.3 0.1 reshape.112
  59.4 0.0 copy-done.8
  59.4 0.3 fusion.14
  59.7 0.0 copy-done.5
  59.7 0.6 fusion.41.refs_4_
  60.3 0.0 copy-done.2
  60.3 2.5 %copy.40 = f32[1,128,8,512]{3,1,2,0:T(8,128)} copy(f32[1,128,8,512]{3,2,1,0:T(8,128)S(1)} %copy-done.2) | data formatting | bytes 4194304 | tf_op args[1]
  62.8 55.9 %shard_map.115 = (f32[8,128,512]{2,1,0:T(8,128)}, f32[8,128,512]{2,1,0:T(8,128)}) custom-call(f32[8,128,512]{2,1,0:T(8,128)} %shard_map.113.refs_0_, f32[8,128,512]{2,1,0:T(8,128)} %get-tuple-element.14.refs_1_, f32[128,128]{1,0:T(8,128)} %bitcast.57, f32[8,512]{1,0:T(8,128)} %convert_select_fusion.refs_3_, f32[8,512]{1,0:T(8,128)} %fusion.41.refs_4_, ...), custom_call_target="tpu_custom_call" | custom-call | tf_op jit(solution)/shard_map/pallas_call | solution.py:244
  118.7 0.9 slice.7
  119.6 0.0 copy-done.4
  119.6 0.2 fusion.12
  119.9 2.9 %fusion.1 = f32[64,128]{1,0:T(8,128)S(1)} fusion(f32[1,64,128,128]{3,2,1,0:T(8,128)} %param.19, f32[64,128]{1,0:T(8,128)S(1)} %fusion.12), kind=kLoop, calls=%fused_computation.3 | loop fusion | flops 2088960 | bytes 4259840 | tf_op jit(solution)/shard_map/reduce_sum | solution.py:359
  122.8 0.9 fusion.10.parcel
  123.6 16.1 %shard_map.116 = f32[16,8,128]{2,1,0:T(8,128)} custom-call(f32[16,8,128]{2,1,0:T(8,128)} %fusion.10.parcel), custom_call_target="tpu_custom_call" | custom-call | tf_op jit(solution)/shard_map/pallas_call | solution.py:284
  139.8 0.1 eq.110
  139.9 0.1 broadcast_in_dim.35
  139.9 0.1 mul.86
  140.0 1.1 fusion.2
  141.2 0.6 reshape.117.refs_4_
  141.8 30.8 %shard_map.117 = f32[8,128,512]{2,1,0:T(8,128)} custom-call(f32[8,128,512]{2,1,0:T(8,128)} %get-tuple-element.5.refs_0_, f32[8,128,512]{2,1,0:T(8,128)} %get-tuple-element.14.refs_1_, f32[128,128]{1,0:T(8,128)} %bitcast.58, f32[8,512]{1,0:T(8,128)} %convert_select_fusion.refs_3_, f32[8,512]{1,0:T(8,128)} %reshape.117.refs_4_), custom_call_target="tpu_custom_call" | custom-call | tf_op jit(solution)/shard_map/pallas_call | solution.py:244
  172.6 0.0 copy-done.1
  172.6 2.9 %bitcast_add_fusion = f32[1,128,8,512]{3,1,2,0:T(8,128)S(1)} fusion(f32[8,128,512]{2,1,0:T(8,128)} %shard_map.117, f32[1,128,8,512]{3,2,1,0:T(8,128)S(1)} %copy-done.1), kind=kLoop, calls=%fused_computation.4 | loop fusion | flops 524288 | bytes 6291456 | tf_op jit(solution)/shard_map/add | solution.py:374
  175.6 2.5 %copy.34 = f32[1,128,8,512]{3,2,1,0:T(8,128)} copy(f32[1,128,8,512]{3,1,2,0:T(8,128)S(1)} %bitcast_add_fusion) | data formatting | bytes 4194304
  178.1 2.5 %copy.33 = f32[1,128,8,512]{3,2,1,0:T(8,128)} copy(f32[1,128,8,512]{3,1,2,0:T(8,128)S(1)} %bitcast.55) | data formatting | bytes 4194304
  (14 shorter events, 0.1 us)
Async XLA Ops:
  0.6 0.7 copy-start
  10.1 44.1 %copy-start.6 = (s32[2,16,8]{1,2,0:T(8,128)S(1)}, s32[2,16,8]{1,2,0:T(8,128)}, u32[]{:S(2)}) copy-start(s32[2,16,8]{1,2,0:T(8,128)} %param.15) | copy-start | bytes 3076
  55.6 3.5 %copy-start.7 = (s32[1,1,8]{2,1,0:T(1,128)S(1)}, s32[1,1,8]{2,1,0:T(1,128)}, u32[]{:S(2)}) copy-start(s32[1,1,8]{2,1,0:T(1,128)} %param.18) | copy-start | bytes 100
  55.6 3.7 %copy-start.8 = (s32[1,1,64]{2,1,0:T(1,128)S(1)}, s32[1,1,64]{2,1,0:T(1,128)}, u32[]{:S(2)}) copy-start(s32[1,1,64]{2,1,0:T(1,128)} %param.17) | copy-start | bytes 772
  55.7 4.0 %copy-start.5 = (s32[8,512]{1,0:T(8,128)S(1)}, s32[8,512]{1,0:T(8,128)}, u32[]{:S(2)}) copy-start(s32[8,512]{1,0:T(8,128)} %param.14) | copy-start | bytes 49156
  55.7 4.6 %copy-start.2 = (f32[1,128,8,512]{3,2,1,0:T(8,128)S(1)}, f32[1,128,8,512]{3,2,1,0:T(8,128)}, u32[]{:S(2)}) copy-start(f32[1,128,8,512]{3,2,1,0:T(8,128)} %param.11) | copy-start | bytes 6291460
  62.8 56.8 %copy-start.4 = (f32[8,512]{1,0:T(8,128)S(1)}, f32[8,512]{1,0:T(8,128)}, u32[]{:S(2)}) copy-start(f32[8,512]{1,0:T(8,128)} %convert_select_fusion.refs_3_) | copy-start | bytes 49156
  141.8 30.8 %copy-start.1 = (f32[1,128,8,512]{3,2,1,0:T(8,128)S(1)}, f32[1,128,8,512]{3,2,1,0:T(8,128)}, u32[]{:S(2)}) copy-start(f32[1,128,8,512]{3,2,1,0:T(8,128)} %param.10) | copy-start | bytes 6291460
  175.6 2.5 %copy-start.3 = (f32[8,128,512]{2,1,0:T(8,128)S(1)}, f32[8,128,512]{2,1,0:T(8,128)}, u32[]{:S(2)}) copy-start(f32[8,128,512]{2,1,0:T(8,128)} %get-tuple-element.4) | copy-start | bytes 6291460

commit v2 on v1

--- a/solution.py
+++ b/solution.py
@@ -8,7 +8,7 @@
 from jax.sharding import PartitionSpec as P
 
 STEPS = 4
-CHUNKS = 2
+CHUNKS = 4
 SUB = 32
 MESH = pl.DeviceIdType.MESH
 precise = lax.Precision.HIGHEST
@@ -33,7 +33,7 @@
     x_hbm, d_ref, a_ref, sea_ref = refs[:4]
     del refs[:4]
     add_ref = refs.pop(0)
-    measured = refs.pop(0) if forward and backward else None
+    extra = refs.pop(0) if backward else None
     outs = [refs.pop(0) for _ in range(bool(forward) + bool(backward))]
     state, halo, send_sem, recv_sem, io_sem, wide, low = refs[:7]
     del refs[:7]
@@ -130,7 +130,7 @@
             _, lap = stencil(now, above, below, k, cols)
             adjoint = masked[r, k, cols] + lap + y[k]
             if last:
-                masked[r, k, cols] = adjoint
+                masked[r, k, cols] = adjoint if forward else adjoint + extra[r, k, cols]
             else:
                 scaled_row(slot + 1, r, cols, k, adjoint)
 
@@ -186,7 +186,7 @@
         def start_row(r, _):
             for k in pieces():
                 if forward:
-                    value = state[forward, r, k, :] - measured[r, k, :]
+                    value = state[forward, r, k, :] - extra[r, k, :]
                 else:
                     value = masked[r, k, :]
                 scaled_row(slot0, r, every, k, value)
@@ -218,13 +218,13 @@
         store.wait()
 
 
-def run_block(tiles, ident, forward, backward, x, d, a, sea, add, measured=None):
+def run_block(tiles, ident, forward, backward, x, d, a, sea, add, extra=None):
     rows, levels, lon = x.shape
     total = forward + backward
     slots = (forward + 1 if forward else 0) + backward
     vmem = pl.BlockSpec(memory_space=pltpu.VMEM)
     hbm = pl.BlockSpec(memory_space=pl.ANY)
-    operands = [x, d, a, sea, add] + ([measured] if measured is not None else [])
+    operands = [x, d, a, sea, add] + ([extra] if extra is not None else [])
     outs = bool(forward) + bool(backward)
     scratch = [
         pltpu.VMEM((slots, rows, levels, lon), f32),
@@ -370,9 +370,9 @@
         vert_mix[0],
         sea,
         returned.reshape(row_count, lon_count),
-    )
-    gradient = starting_perturbation + jnp.swapaxes(last, 0, 1)[None]
-    return (jnp.swapaxes(final, 0, 1)[None], gradient)
+        start,
+    )
+    return (jnp.swapaxes(final, 0, 1)[None], jnp.swapaxes(last, 0, 1)[None])
 
 
 def solution(mesh):

time: 181 us -> 171 us (0.945)
  Pallas kernels: 145 us -> 136 us
  other arithmetic: 12.2 us -> 9.21 us
    pallas_call x2, Pallas kernels: 26.8 us -> 18.5 us  [swap(): pl.pallas_call(functools.partial(swap_kernel, tiles), out_shape=jax.Shape...]
    add x1 -> x0, other arithmetic: 2.94 us -> none  [shards(): gradient = starting_perturbation + jnp.swapaxes(last, 0, 1)[None]]
    unnamed x22 -> x20, local copies, waits for them, and re-layouts: 7.75 us -> 9.51 us
where the time goes in v2:
time: 171 us
  Pallas kernels  136 us (80%)
  local copies, waits for them, and re-layouts  19.8 us (12%)
  other arithmetic  9.21 us (5%)
  matrix products  4.45 us (3%)
    pallas_call x3, Pallas kernels, run_block(): pl.pallas_call(functools.partial(block, tiles, forward, backward), out_sh...  118 us
    pallas_call x2, Pallas kernels, swap(): pl.pallas_call(functools.partial(swap_kernel, tiles), out_shape=jax.Shape...  18.5 us
    unnamed x20, local copies, waits for them, and re-layouts  9.51 us
    transpose x1, local copies, waits for them, and re-layouts, to_rows(): return jnp.swapaxes(x[0], 0, 1)  6.66 us
    reduce_sum x1, other arithmetic, shards(): terms = jnp.sum(weights * picked[:, None, :], axis=2)  3.49 us

profile of v2, /device:TPU:1, one launch (start us, length us, event | category | flops | bytes accessed | tf_op | source)
XLA Modules:
  0.0 170.5 jit_solution(333351701847489958)
XLA Ops:
  0.6 0.0 copy-start
  0.7 0.7 convert_bitcast_fusion
  1.3 0.0 copy-done
  1.4 0.1 copy.32
  1.5 0.1 copy.27
  1.6 1.3 convert_select_fusion.refs_3_
  2.9 6.7 %copy_bitcast_fusion.1 = (f32[8,128,512]{2,1,0:T(8,128)}, f32[8,128,512]{2,1,0:T(8,128)}) fusion(f32[1,128,8,512]{3,2,1,0:T(8,128)} %param.12, f32[1,128,8,512]{3,2,1,0:T(8,128)} %param.10), kind=kLoop, calls=%fused_computation.5 | loop fusion | bytes 8388608 | tf_op jit(solution)/shard_map/transpose | solution.py:339
  9.5 0.6 broadcast_in_dim.31.refs_4_
  10.1 31.3 %shard_map.113.refs_0_ = f32[8,128,512]{2,1,0:T(8,128)} custom-call(f32[8,128,512]{2,1,0:T(8,128)} %get-tuple-element.15.refs_0_.refs_5_, f32[8,128,512]{2,1,0:T(8,128)} %get-tuple-element.14.refs_1_, f32[128,128]{1,0:T(8,128)} %bitcast.56, f32[8,512]{1,0:T(8,128)} %convert_select_fusion.refs_3_, f32[8,512]{1,0:T(8,128)} %broadcast_in_dim.31.refs_4_), custom_call_target="tpu_custom_call" | custom-call | tf_op jit(solution)/shard_map/pallas_call | solution.py:244
  41.5 0.9 slice.6
  42.4 0.9 fusion.6.parcel
  43.3 9.7 %shard_map.114 = f32[16,8,128]{2,1,0:T(8,128)} custom-call(f32[16,8,128]{2,1,0:T(8,128)} %fusion.6.parcel), custom_call_target="tpu_custom_call" | custom-call | tf_op jit(solution)/shard_map/pallas_call | solution.py:284
  53.0 0.0 copy-done.5
  53.0 0.2 multiply_reduce_fusion
  53.2 0.1 broadcast_in_dim.33
  53.3 0.1 mul.77
  53.4 1.1 fusion.4
  54.5 0.0 copy-start.6
  54.5 0.0 copy-start.7
  54.5 0.0 copy-start.4
  54.5 0.0 copy-start.1
  54.5 3.5 %fusion = f32[64,128]{1,0:T(8,128)S(1)} fusion(f32[1,64,128,128]{3,2,1,0:T(8,128)} %param.19, f32[64,128]{1,0:T(8,128)S(1)} %fusion.4), kind=kLoop, calls=%fused_computation.2 | loop fusion | flops 2088960 | bytes 4259840 | tf_op jit(solution)/shard_map/reduce_sum | solution.py:351
  58.0 0.0 copy-done.6
  58.0 0.1 broadcast_in_dim.32
  58.1 0.1 reshape.112
  58.2 0.0 copy-done.7
  58.2 0.3 fusion.14
  58.5 0.0 copy-done.4
  58.5 0.6 fusion.41.refs_4_
  59.1 0.0 copy-done.1
  59.1 2.6 %copy.36 = f32[1,128,8,512]{3,1,2,0:T(8,128)} copy(f32[1,128,8,512]{3,2,1,0:T(8,128)S(1)} %copy-done.1) | data formatting | bytes 4194304 | tf_op args[1]
  61.7 55.5 %shard_map.115 = (f32[8,128,512]{2,1,0:T(8,128)}, f32[8,128,512]{2,1,0:T(8,128)}) custom-call(f32[8,128,512]{2,1,0:T(8,128)} %shard_map.113.refs_0_, f32[8,128,512]{2,1,0:T(8,128)} %get-tuple-element.14.refs_1_, f32[128,128]{1,0:T(8,128)} %bitcast.57, f32[8,512]{1,0:T(8,128)} %convert_select_fusion.refs_3_, f32[8,512]{1,0:T(8,128)} %fusion.41.refs_4_, ...), custom_call_target="tpu_custom_call" | custom-call | tf_op jit(solution)/shard_map/pallas_call | solution.py:244
  117.1 0.9 slice.7
  118.1 0.0 copy-done.3
  118.1 0.2 fusion.12
  118.3 2.9 %fusion.1 = f32[64,128]{1,0:T(8,128)S(1)} fusion(f32[1,64,128,128]{3,2,1,0:T(8,128)} %param.19, f32[64,128]{1,0:T(8,128)S(1)} %fusion.12), kind=kLoop, calls=%fused_computation.3 | loop fusion | flops 2088960 | bytes 4259840 | tf_op jit(solution)/shard_map/reduce_sum | solution.py:359
  121.2 0.9 fusion.10.parcel
  122.1 8.7 %shard_map.116 = f32[16,8,128]{2,1,0:T(8,128)} custom-call(f32[16,8,128]{2,1,0:T(8,128)} %fusion.10.parcel), custom_call_target="tpu_custom_call" | custom-call | tf_op jit(solution)/shard_map/pallas_call | solution.py:284
  130.8 0.1 eq.110
  130.9 0.1 broadcast_in_dim.35
  130.9 0.1 mul.86
  131.0 1.1 fusion.2
  132.2 0.6 reshape.117.refs_4_
  132.8 30.9 %shard_map.117 = f32[8,128,512]{2,1,0:T(8,128)} custom-call(f32[8,128,512]{2,1,0:T(8,128)} %get-tuple-element.5.refs_0_, f32[8,128,512]{2,1,0:T(8,128)} %get-tuple-element.14.refs_1_, f32[128,128]{1,0:T(8,128)} %bitcast.58, f32[8,512]{1,0:T(8,128)} %convert_select_fusion.refs_3_, f32[8,512]{1,0:T(8,128)} %reshape.117.refs_4_, ...), custom_call_target="tpu_custom_call" | custom-call | tf_op jit(solution)/shard_map/pallas_call | solution.py:244
  163.7 0.0 copy-start.2
  163.7 4.3 %copy.31 = f32[1,128,8,512]{3,2,1,0:T(8,128)} copy(f32[1,128,8,512]{3,1,2,0:T(8,128)} %bitcast.54) | data formatting | bytes 4194304
  168.0 0.0 copy-done.2
  168.0 2.5 %copy.30 = f32[1,128,8,512]{3,2,1,0:T(8,128)} copy(f32[1,128,8,512]{3,1,2,0:T(8,128)S(1)} %bitcast.55) | data formatting | bytes 4194304
  (11 shorter events, 0.1 us)
Async XLA Ops:
  0.6 0.7 copy-start
  10.1 42.9 %copy-start.5 = (s32[2,16,8]{1,2,0:T(8,128)S(1)}, s32[2,16,8]{1,2,0:T(8,128)}, u32[]{:S(2)}) copy-start(s32[2,16,8]{1,2,0:T(8,128)} %param.15) | copy-start | bytes 3076
  54.5 3.5 %copy-start.6 = (s32[1,1,8]{2,1,0:T(1,128)S(1)}, s32[1,1,8]{2,1,0:T(1,128)}, u32[]{:S(2)}) copy-start(s32[1,1,8]{2,1,0:T(1,128)} %param.18) | copy-start | bytes 100
  54.5 3.7 %copy-start.7 = (s32[1,1,64]{2,1,0:T(1,128)S(1)}, s32[1,1,64]{2,1,0:T(1,128)}, u32[]{:S(2)}) copy-start(s32[1,1,64]{2,1,0:T(1,128)} %param.17) | copy-start | bytes 772
  54.5 4.0 %copy-start.4 = (s32[8,512]{1,0:T(8,128)S(1)}, s32[8,512]{1,0:T(8,128)}, u32[]{:S(2)}) copy-start(s32[8,512]{1,0:T(8,128)} %param.14) | copy-start | bytes 49156
  54.5 4.6 %copy-start.1 = (f32[1,128,8,512]{3,2,1,0:T(8,128)S(1)}, f32[1,128,8,512]{3,2,1,0:T(8,128)}, u32[]{:S(2)}) copy-start(f32[1,128,8,512]{3,2,1,0:T(8,128)} %param.11) | copy-start | bytes 6291460
  61.7 56.4 %copy-start.3 = (f32[8,512]{1,0:T(8,128)S(1)}, f32[8,512]{1,0:T(8,128)}, u32[]{:S(2)}) copy-start(f32[8,512]{1,0:T(8,128)} %convert_select_fusion.refs_3_) | copy-start | bytes 49156
  163.7 4.3 %copy-start.2 = (f32[8,128,512]{2,1,0:T(8,128)S(1)}, f32[8,128,512]{2,1,0:T(8,128)}, u32[]{:S(2)}) copy-start(f32[8,128,512]{2,1,0:T(8,128)} %get-tuple-element.4) | copy-start | bytes 6291460
